TPU v7x, 256 devices: a 2x2x32 block of a 4x8x32 slice. The times are simulated.
256 devices in a mesh: member: 4 (over y, x), gx: 64 (over z, core).
Axes of the slice: x: 2, y: 2, z: 32, core: 2. Of those that a mesh axis runs over, the one named last changes fastest.
The devices are a block of a 4x8x32 slice.
Arguments:
- spectrum: float32 [36, 32, 2048, 128], P(None, None, ('member', 'gx')), parts along dimension 2, may hold values from 0 to 1
- wind: float32 [2, 2048, 128], P(None, ('member', 'gx')), parts along dimension 1, may hold values from -32 to 32
- land_sea: int32 [512, 128], P('gx'), may hold values 0 or 1
- band_rows: int32 [128], replicated, may hold values from 0 to 127, each once
Outputs:
- spectrum_next: float32 [36, 32, 2048, 128], P(None, None, ('member', 'gx')), parts along dimension 2
- ocean_fields: float32 [4, 128, 2048], P(None, 'gx', 'member'), parts along dimension 2
There are 4 independent parts, one for each index of `member`. A program takes and returns all parts, laid end to end along the dimension named above; an argument that names none is the same for every part. Nothing has to cross between parts.
Inputs may be any that keep to these rules, and one draw needn't show every extreme that they name: band_rows names each of the 128 latitude rows exactly once.
All inputs are finite; a program needn't handle non-finite values. No bound on the sum of `land_sea` on one device may be relied on, other than what follows from the above.
Results may differ from a plain program's by a relative error of at most 0.00015.
Values sent between devices are 32-bit elements; how exact they have to be, the bound alone decides.
A program may use at most 128 MiB of HBM per device.

v0:
```python
import math

import jax
import jax.numpy as jnp
from jax import lax
from jax.sharding import Mesh
from jax.sharding import PartitionSpec as P

STEPS = 3
GX = ("gx_0", "gx_1")
MEMBER_GX = ("member", "gx_0", "gx_1")


def passed_along(value, axis, steps):
    count = lax.axis_size(axis)
    pairs = [(source, (source + steps) % count) for source in range(count)]
    return lax.ppermute(value, axis, pairs)


def in_blocks(shard, dim, devices):
    before, after = (shard.shape[:dim], shard.shape[dim + 1 :])
    return jnp.moveaxis(shard.reshape(*before, devices, -1, *after), dim, 0)


def laid_out(blocks, dim):
    blocks = jnp.moveaxis(blocks, 0, dim)
    lengths = blocks.shape
    return blocks.reshape(*lengths[:dim], lengths[dim] * lengths[dim + 1], *lengths[dim + 2 :])


def moved_by_axis(blocks, axes, turns):
    inside = blocks.shape[1:]
    out = blocks.reshape(*(lax.axis_size(a) for a in axes), *inside)
    for k in turns:
        out = lax.all_to_all(out, axes[k], k, k, tiled=True)
    return out.reshape(-1, *inside)


def exchange_by_chip(shard, groups, turns, split_dim, concat_dim):
    devices = lax.axis_size(groups[0]) * lax.axis_size(groups[1])
    blocks = in_blocks(shard, split_dim, devices)
    return laid_out(moved_by_axis(blocks, groups, turns), concat_dim)


def wave_tables(directions, frequencies):
    angles = (jnp.arange(directions, dtype=jnp.float32) + 0.5) * (2.0 * math.pi / directions)
    levels = jnp.arange(frequencies, dtype=jnp.float32)
    shrink = jnp.power(jnp.float32(1.1), -levels)
    frequency = 0.0418 / shrink
    inverse_speed = 2.0 * math.pi * frequency / 9.81
    weight = (levels + 1.0) / frequencies
    cosine_dir = jnp.cos(angles)[:, None]
    sine_dir = jnp.sin(angles)[:, None]
    courant_x = 0.45 * shrink[None, :] * cosine_dir
    courant_y = 0.45 * shrink[None, :] * sine_dir
    factor = 3.0 / math.sqrt(directions * frequencies)
    project = jnp.stack(
        [factor * weight[None, :] * cosine_dir, factor * weight[None, :] * sine_dir]
    )
    return (courant_x, courant_y, cosine_dir, sine_dir, inverse_speed, weight * weight, project)


def upwind(center, west_cell, east_cell, courant_x, courant_y):
    along_x = courant_x[:, :, None, None]
    along_y = courant_y[:, :, None, None]
    border = jnp.zeros_like(center[..., :1])
    south_cell = jnp.concatenate([border, center[..., :-1]], axis=3)
    north_cell = jnp.concatenate([center[..., 1:], border], axis=3)
    return (
        center
        - jnp.maximum(along_x, 0.0) * (center - west_cell)
        + jnp.maximum(-along_x, 0.0) * (east_cell - center)
        - jnp.maximum(along_y, 0.0) * (center - south_cell)
        + jnp.maximum(-along_y, 0.0) * (north_cell - center)
    )


def sources(advected, wind_east, wind_north, sea_mask, tables):
    cosine_dir, sine_dir, inverse_speed, weight_two = (tables[2], tables[3], tables[4], tables[5])
    advected = advected * sea_mask
    energy = jnp.mean(advected, axis=(0, 1))
    wind_ratio = (
        wind_east * cosine_dir[:, :, None, None] + wind_north * sine_dir[:, :, None, None]
    ) * inverse_speed[None, :, None, None]
    growth = 0.05 * jnp.clip(wind_ratio - 1.0, 0.0, 4.0)
    damping = 0.3 * weight_two[None, :, None, None] * (energy / (0.5 + energy))
    return (advected * (1.0 + growth) / (1.0 + damping), growth * advected)


def coupling_fields(input_flux, current, project):
    stress = jnp.einsum("cij,ijxy->cxy", project, input_flux, precision=lax.Precision.HIGHEST)
    stokes = jnp.einsum("cij,ijxy->cxy", project, current, precision=lax.Precision.HIGHEST)
    return jnp.concatenate([stress, stokes], axis=0)


def per_device(spectrum, wind, land_sea, band_rows):
    tables = wave_tables(spectrum.shape[0], spectrum.shape[1])
    sea_mask = land_sea.astype(jnp.float32)
    current = spectrum
    quarter = spectrum.shape[0] // 4
    east_x = jnp.concatenate([tables[0][:quarter], tables[0][3 * quarter :]], axis=0)
    east_y = jnp.concatenate([tables[1][:quarter], tables[1][3 * quarter :]], axis=0)
    west_x = tables[0][quarter : 3 * quarter]
    west_y = tables[1][quarter : 3 * quarter]
    for step_index in range(STEPS):
        eastward = jnp.concatenate([current[:quarter], current[3 * quarter :]], axis=0)
        westward = current[quarter : 3 * quarter]
        from_west = passed_along(eastward[:, :, -1:], GX, 1)
        from_east = passed_along(westward[:, :, :1], GX, -1)
        west_cells = jnp.concatenate([from_west, eastward[:, :, :-1]], axis=2)
        east_cells = jnp.concatenate([westward[:, :, 1:], from_east], axis=2)
        moved_east = upwind(eastward, west_cells, eastward, east_x, east_y)
        moved_west = upwind(westward, westward, east_cells, west_x, west_y)
        advected = jnp.concatenate([moved_east[:quarter], moved_west, moved_east[quarter:]], axis=0)
        current, input_flux = sources(advected, wind[0], wind[1], sea_mask, tables)
    fields = coupling_fields(input_flux, current, tables[6])
    local_rows = jnp.transpose(fields[:, :, band_rows], (0, 2, 1))
    ocean_fields = exchange_by_chip(local_rows, ("gx_0", "gx_1"), (1, 0), 1, 2)
    return (current, ocean_fields)


def solution(mesh):
    torus = Mesh(mesh.devices.reshape(mesh.shape["member"], 32, 2), ("member", "gx_0", "gx_1"))
    placed = (P(None, None, MEMBER_GX, None), P(None, MEMBER_GX, None), P(GX, None), P())
    return jax.shard_map(
        per_device,
        mesh=torus,
        in_specs=placed,
        out_specs=(P(None, None, MEMBER_GX, None), P(None, GX, "member")),
        check_vma=False,
    )
```

profile of v0, /device:TPU:37, one launch (start us, length us, event | category | flops | bytes accessed | tf_op | source)
XLA Modules:
  0.0 126.7 jit_solution(18188657073546846578)
XLA Ops:
  0.6 1.8 %fusion.60 = (f32[9,32,8,128]{3,2,1,0:T(8,128)S(1)}, f32[9,32,8,128]{3,2,1,0:T(8,128)S(1)}) fusion(f32[36,32,8,128]{3,2,1,0:T(8,128)} %param.4), kind=kLoop, calls=%fused_computation.120 | loop fusion | bytes 4718592 | tf_op jit(solution)/shard_map/slice | solution.py:106
  2.9 0.7 slice.228
  3.6 3.1 %collective-permute-start = (f32[18,32,1,128]{3,1,2,0:T(8,128)}, f32[18,32,1,128]{3,1,2,0:T(8,128)S(1)}, u32[]{:S(2)}, u32[]{:S(2)}) collective-permute-start(f32[18,32,1,128]{3,1,2,0:T(8,128)} %slice.228), channel_id=1, source_target_pairs={{0,1},{1,2},{2,3},{3,4},{4,5},{5,6},{6,7},{7,8},{8,9},{9,10},{10,1... | collective-permute-start | bytes 884744 | tf_op jit(solution)/shard_map/ppermute | solution.py:17
  6.9 18.6 %collective-permute-start.1 = (f32[18,32,1,128]{3,1,2,0:T(8,128)S(1)}, f32[18,32,1,128]{3,1,2,0:T(8,128)S(1)}, u32[]{:S(2)}, u32[]{:S(2)}) collective-permute-start(f32[18,32,1,128]{3,1,2,0:T(8,128)S(1)} %bitcast.36), channel_id=1, source_target_pairs={{0,63},{1,0},{2,1},{3,2},{4,3},{5,4},{6,5},{7,6},{8,7},{9,8},{10,9... | collective-permute-start | bytes 884744 | tf_op jit(solution)/shard_map/ppermute | solution.py:17
  25.6 3.1 %fusion.64 = (f32[18,32,8,127]{3,1,2,0:T(8,128)}, f32[18,32,8,127]{3,1,2,0:T(8,128)}) fusion(f32[18,32,8,128]{3,1,2,0:T(8,128)S(1)} %copy_dynamic-update-slice_fusion), kind=kLoop, calls=%fused_computation.124 | loop fusion | bytes 9363456 | tf_op jit(solution)/shard_map/slice | solution.py:67
  28.7 1.6 %slice.229 = f32[18,32,7,128]{3,1,2,0:T(8,128)} slice(f32[18,32,8,128]{3,1,2,0:T(8,128)S(1)} %copy_dynamic-update-slice_fusion), slice={[0:18], [0:32], [0:7], [0:128]} | slice | bytes 4128768 | tf_op jit(solution)/shard_map/slice | solution.py:110
  30.4 0.8 fusion.59
  31.3 0.2 slice.190
  31.5 1.9 %copy.77 = f32[18,32,8,127]{3,1,2,0:T(8,128)} copy(f32[18,32,8,127]{3,2,1,0:T(8,128)S(1)} %get-tuple-element.18) | data formatting | bytes 4681728
  33.4 1.8 %copy.78 = f32[18,32,8,127]{3,1,2,0:T(8,128)} copy(f32[18,32,8,127]{3,2,1,0:T(8,128)S(1)} %get-tuple-element.19) | data formatting | bytes 4681728
  35.2 1.7 %copy.75 = f32[18,32,7,128]{3,1,2,0:T(8,128)} copy(f32[18,32,7,128]{3,2,1,0:T(8,128)S(1)} %slice.190) | data formatting | bytes 4128768
  37.3 4.1 %fusion.16 = f32[18,32,8,128]{3,1,2,0:T(8,128)S(1)} fusion(f32[18,32,8,128]{3,1,2,0:T(8,128)S(1)} %copy_dynamic-update-slice_fusion, f32[18,32,7,128]{3,1,2,0:T(8,128)} %slice.229, f32[18,32,1,128]{3,1,2,0:T(8,128)S(1)} %collective-permute-done, f32[18,32,8,127]{3,1,2,0:T(8,128)} %get-tuple-element.33, f32[18,32,8,127]{3,1,2,0:T(8,128)} %get-tuple-element.32, ...), kind=kLoop, calls=%fused_computation.43 | loop fusion | flops 7667712 | bytes 11768832 | tf_op jit(solution)/shard_map/add | solution.py:70
  41.5 0.3 fusion.63
  41.8 1.3 %slice-done = f32[18,32,8,128]{3,2,1,0:T(8,128)S(1)} async-done(((f32[36,32,8,128]{3,2,1,0:T(8,128)}), f32[18,32,8,128]{3,2,1,0:T(8,128)S(1)}, s32[]{:S(2)}) %slice-start) | async-done | bytes 2359320 | tf_op jit(solution)/shard_map/slice | solution.py:107
  43.2 0.7 copy-done.2
  43.9 1.7 %fusion.20 = f32[18,32,8,128]{3,1,2,0:T(8,128)S(1)} fusion(f32[18,32,1,128]{3,1,2,0:T(8,128)S(1)} %collective-permute-done.1, f32[18,32,7,128]{3,1,2,0:T(8,128)S(1)} %copy-done.4, f32[18,32,8,127]{3,1,2,0:T(8,128)S(1)} %copy-done.3, f32[18,32,8,127]{3,1,2,0:T(8,128)S(1)} %copy-done.2, f32[18,32,8,128]{3,2,1,0:T(8,128)S(1)} %slice-done, ...), kind=kLoop, calls=%fused_computation.48 | loop fusion | flops 7667712 | bytes 11768832 | tf_op jit(solution)/shard_map/add | solution.py:70
  45.6 0.6 fusion.7
  46.3 1.4 %multiply_divide_fusion.2 = f32[36,32,8,128]{3,1,2,0:T(8,128)S(1)} fusion(f32[9,32,8,128]{3,1,2,0:T(8,128)S(1)} %get-tuple-element.31, f32[18,32,8,128]{3,1,2,0:T(8,128)S(1)} %fusion.20, f32[9,32,8,128]{3,1,2,0:T(8,128)S(1)} %get-tuple-element.30, f32[32,8,128]{2,0,1:T(8,128)S(1)} %multiply_add_fusion.3, f32[32]{0:T(128)S(1)} %power_multiply_fusion, ...), kind=kLoop, calls=%fused_computation.10 | loop fusion | flops 11796480 | bytes 9719936 | tf_op jit(solution)/shard_map/div | solution.py:87
  47.7 0.9 fusion.57
  48.6 0.3 fusion.58
  49.5 3.6 %collective-permute-start.3 = (f32[18,32,1,128]{3,1,2,0:T(8,128)S(1)}, f32[18,32,1,128]{3,1,2,0:T(8,128)S(1)}, u32[]{:S(2)}, u32[]{:S(2)}) collective-permute-start(f32[18,32,1,128]{3,1,2,0:T(8,128)S(1)} %slice.251), channel_id=1, source_target_pairs={{0,63},{1,0},{2,1},{3,2},{4,3},{5,4},{6,5},{7,6},{8,7},{9,8},{10,9... | collective-permute-start | bytes 884744 | tf_op jit(solution)/shard_map/ppermute | solution.py:17
  53.1 0.9 fusion.10
  54.0 1.9 %fusion.25 = f32[18,32,8,128]{3,1,2,0:T(8,128)S(1)} fusion(f32[18,32,7,128]{3,1,2,0:T(8,128)S(1)} %fusion.40, f32[18,32,1,128]{3,1,2,0:T(8,128)S(1)} %collective-permute-done.2, f32[18,32,8,127]{3,1,2,0:T(8,128)S(1)} %get-tuple-element.29, f32[18,32,8,127]{3,1,2,0:T(8,128)S(1)} %get-tuple-element.28, f32[9,32,8,128]{3,1,2,0:T(8,128)S(1)} %get-tuple-element.16, ...), kind=kLoop, calls=%fused_computation.54 | loop fusion | flops 8257536 | bytes 11768832 | tf_op jit(solution)/shard_map/add | solution.py:70
  56.1 1.8 %fusion.29 = f32[18,32,8,128]{3,1,2,0:T(8,128)S(1)} fusion(f32[18,32,1,128]{3,1,2,0:T(8,128)S(1)} %collective-permute-done.3, f32[18,32,7,128]{3,1,2,0:T(8,128)S(1)} %slice.250, f32[18,32,8,127]{3,1,2,0:T(8,128)S(1)} %get-tuple-element.15, f32[18,32,8,127]{3,1,2,0:T(8,128)S(1)} %get-tuple-element.14, f32[36,32,8,128]{3,1,2,0:T(8,128)S(1)} %multiply_divide_fusion.2, ...), kind=kLoop, calls=%fused_computation.59 | loop fusion | flops 7667712 | bytes 11768832 | tf_op jit(solution)/shard_map/add | solution.py:70
  57.9 0.6 fusion.6
  58.6 1.4 %multiply_divide_fusion.1 = f32[36,32,8,128]{3,1,2,0:T(8,128)S(1)} fusion(f32[9,32,8,128]{3,1,2,0:T(8,128)S(1)} %get-tuple-element.27, f32[18,32,8,128]{3,1,2,0:T(8,128)S(1)} %fusion.29, f32[9,32,8,128]{3,1,2,0:T(8,128)S(1)} %get-tuple-element.26, f32[32,8,128]{2,0,1:T(8,128)S(1)} %multiply_add_fusion.2, f32[32]{0:T(128)S(1)} %power_multiply_fusion, ...), kind=kLoop, calls=%fused_computation.9 | loop fusion | flops 11796480 | bytes 9719936 | tf_op jit(solution)/shard_map/div | solution.py:87
  60.0 0.9 fusion.55
  60.9 0.3 fusion.56
  61.2 1.2 collective-permute-start.4
  62.9 4.8 %collective-permute-start.5 = (f32[18,32,1,128]{3,1,2,0:T(8,128)S(1)}, f32[18,32,1,128]{3,1,2,0:T(8,128)S(1)}, u32[]{:S(2)}, u32[]{:S(2)}) collective-permute-start(f32[18,32,1,128]{3,1,2,0:T(8,128)S(1)} %slice.268), channel_id=1, source_target_pairs={{0,63},{1,0},{2,1},{3,2},{4,3},{5,4},{6,5},{7,6},{8,7},{9,8},{10,9... | collective-permute-start | bytes 884744 | tf_op jit(solution)/shard_map/ppermute | solution.py:17
  67.7 0.9 fusion.8
  68.6 2.2 %fusion.34 = f32[18,32,8,128]{3,1,2,0:T(8,128)S(1)} fusion(f32[18,32,7,128]{3,1,2,0:T(8,128)S(1)} %fusion.39, f32[18,32,1,128]{3,1,2,0:T(8,128)S(1)} %collective-permute-done.4, f32[18,32,8,127]{3,1,2,0:T(8,128)S(1)} %get-tuple-element.25, f32[18,32,8,127]{3,1,2,0:T(8,128)S(1)} %get-tuple-element.24, f32[9,32,8,128]{3,1,2,0:T(8,128)S(1)} %get-tuple-element.12, ...), kind=kLoop, calls=%fused_computation.65 | loop fusion | flops 8257536 | bytes 11768832 | tf_op jit(solution)/shard_map/add | solution.py:70
  71.0 1.8 %fusion.38 = f32[18,32,8,128]{3,1,2,0:T(8,128)S(1)} fusion(f32[18,32,1,128]{3,1,2,0:T(8,128)S(1)} %collective-permute-done.5, f32[18,32,7,128]{3,1,2,0:T(8,128)S(1)} %slice.267, f32[18,32,8,127]{3,1,2,0:T(8,128)S(1)} %get-tuple-element.11, f32[18,32,8,127]{3,1,2,0:T(8,128)S(1)} %get-tuple-element.10, f32[36,32,8,128]{3,1,2,0:T(8,128)S(1)} %multiply_divide_fusion.1, ...), kind=kLoop, calls=%fused_computation.70 | loop fusion | flops 7667712 | bytes 11768832 | tf_op jit(solution)/shard_map/add | solution.py:70
  72.8 0.6 fusion.41
  73.5 1.6 %fusion.4 = (f32[36,32,8,128]{3,1,2,0:T(8,128)S(1)}, f32[36,32,8,128]{3,1,2,0:T(8,128)S(1)}) fusion(f32[32]{0:T(128)S(1)} %power_multiply_fusion, f32[36,8,128]{2,1,0:T(8,128)S(1)} %multiply_add_fusion, f32[8,128]{1,0:T(8,128)S(1)} %convert_element_type.3, f32[9,32,8,128]{3,1,2,0:T(8,128)S(1)} %get-tuple-element.23, f32[18,32,8,128]{3,1,2,0:T(8,128)S(1)} %fusion.38, ...), kind=kLoop, calls=%fused_computation.12 | loop fusion | flops 12976128 | bytes 14438528 | tf_op jit(solution)/shard_map/mul | solution.py:87
  75.0 2.4 %fusion.42 = f32[2,8,128]{2,0,1:T(2,128)S(1)} fusion(f32[2,36,32,1]{2,0,1,3:T(2,128)S(1)} %copy.60, f32[36,32,8,128]{3,1,2,0:T(8,128)S(1)} %get-tuple-element.8), kind=kOutput, calls=%fused_computation.76 | convolution fusion | flops 28311552 | bytes 4736000 | tf_op jit(solution)/shard_map/cij,ijxy->cxy/dot_general | solution.py:91
  77.4 2.4 %fusion.45 = f32[2,8,128]{2,0,1:T(2,128)S(1)} fusion(f32[2,36,32,1]{2,0,1,3:T(2,128)S(1)} %copy.60, f32[36,32,8,128]{3,1,2,0:T(8,128)S(1)} %get-tuple-element.9), kind=kOutput, calls=%fused_computation.77 | convolution fusion | flops 28311552 | bytes 4736000 | tf_op jit(solution)/shard_map/cij,ijxy->cxy/dot_general | solution.py:92
  80.0 0.8 gather_fusion
  81.1 9.1 %all_to_all.10 = f32[2,1,2048]{2,1,0:T(1,128)S(1)} all-to-all(f32[2,1,2048]{2,1,0:T(1,128)S(1)} %reshape.293), channel_id=1, replica_groups=mesh['member'=4,'gx_0'=32,'gx_1'=2] {'gx_1'}, dimensions={0} | all-to-all | bytes 32768 | tf_op jit(solution)/shard_map/all_to_all | solution.py:35
  90.1 0.5 broadcast.374
  90.7 0.7 reduce
  91.7 1.0 reshape.295
  92.7 11.8 %all-to-all-start.1 = ((f32[32,1,128]{2,1,0:T(1,128)}), f32[32,1,128]{2,1,0:T(1,128)S(1)}, u32[]{:S(2)}, u32[]{:S(2)}) async-start(f32[32,1,128]{2,1,0:T(1,128)} %reshape.295), calls=%async_computation.1 | async-start | bytes 32768 | tf_op jit(solution)/shard_map/all_to_all | solution.py:35
  104.5 8.9 %copy.59 = f32[36,32,8,128]{3,2,1,0:T(8,128)} copy(f32[36,32,8,128]{3,1,2,0:T(8,128)} %copy-done) | data formatting | bytes 9437184
  113.3 11.4 %all-to-all-done.1 = f32[32,1,128]{2,1,0:T(1,128)S(1)} async-done(((f32[32,1,128]{2,1,0:T(1,128)}), f32[32,1,128]{2,1,0:T(1,128)S(1)}, u32[]{:S(2)}, u32[]{:S(2)}) %all-to-all-start.1) | async-done | bytes 16416 | tf_op jit(solution)/shard_map/all_to_all | solution.py:35
  124.8 0.6 reduce.1
  125.4 0.4 reshape.296
  126.0 0.8 reshape.279
  (70 shorter events, 3.9 us)
Async XLA Ops:
  2.4 4.3 %copy-start.1 = (f32[36,32,8,128]{3,2,1,0:T(8,128)S(1)}, f32[36,32,8,128]{3,2,1,0:T(8,128)}, u32[]{:S(2)}) copy-start(f32[36,32,8,128]{3,2,1,0:T(8,128)} %param.4) | copy-start | bytes 14155780
  3.6 33.7 %collective-permute-start = (f32[18,32,1,128]{3,1,2,0:T(8,128)}, f32[18,32,1,128]{3,1,2,0:T(8,128)S(1)}, u32[]{:S(2)}, u32[]{:S(2)}) collective-permute-start(f32[18,32,1,128]{3,1,2,0:T(8,128)} %slice.228), channel_id=1, source_target_pairs={{0,1},{1,2},{2,3},{3,4},{4,5},{5,6},{6,7},{7,8},{8,9},{9,10},{10,1... | collective-permute-start | bytes 884744 | tf_op jit(solution)/shard_map/ppermute | solution.py:17
  6.9 34.9 %collective-permute-start.1 = (f32[18,32,1,128]{3,1,2,0:T(8,128)S(1)}, f32[18,32,1,128]{3,1,2,0:T(8,128)S(1)}, u32[]{:S(2)}, u32[]{:S(2)}) collective-permute-start(f32[18,32,1,128]{3,1,2,0:T(8,128)S(1)} %bitcast.36), channel_id=1, source_target_pairs={{0,63},{1,0},{2,1},{3,2},{4,3},{5,4},{6,5},{7,6},{8,7},{9,8},{10,9... | collective-permute-start | bytes 884744 | tf_op jit(solution)/shard_map/ppermute | solution.py:17
  35.2 1.7 %copy-start.6 = (s32[8,128]{1,0:T(8,128)S(1)}, s32[8,128]{1,0:T(8,128)}, u32[]{:S(2)}) copy-start(s32[8,128]{1,0:T(8,128)} %param.6) | copy-start | bytes 12292
  35.2 1.7 %copy-start.5 = (f32[2,8,128]{2,1,0:T(8,128)S(1)}, f32[2,8,128]{2,1,0:T(8,128)}, u32[]{:S(2)}) copy-start(f32[2,8,128]{2,1,0:T(8,128)} %param.5) | copy-start | bytes 24580
  35.2 1.9 %copy-start.7 = (s32[128]{0:T(128)S(1)}, s32[128]{0:T(128)}, u32[]{:S(2)}) copy-start(s32[128]{0:T(128)} %param.7) | copy-start | bytes 1540
  37.3 4.5 %copy-start.3 = (f32[18,32,8,127]{3,1,2,0:T(8,128)S(1)}, f32[18,32,8,127]{3,1,2,0:T(8,128)}, u32[]{:S(2)}) copy-start(f32[18,32,8,127]{3,1,2,0:T(8,128)} %copy.78) | copy-start | bytes 7022596
  37.3 4.5 %copy-start.4 = (f32[18,32,7,128]{3,1,2,0:T(8,128)S(1)}, f32[18,32,7,128]{3,1,2,0:T(8,128)}, u32[]{:S(2)}) copy-start(f32[18,32,7,128]{3,1,2,0:T(8,128)} %copy.75) | copy-start | bytes 6193156
  41.5 1.7 %slice-start = ((f32[36,32,8,128]{3,2,1,0:T(8,128)}), f32[18,32,8,128]{3,2,1,0:T(8,128)S(1)}, s32[]{:S(2)}) async-start(f32[36,32,8,128]{3,2,1,0:T(8,128)} %param.4), calls=%async_computation.2 | async-start | bytes 4718592 | tf_op jit(solution)/shard_map/slice | solution.py:107
  41.5 2.4 %copy-start.2 = (f32[18,32,8,127]{3,1,2,0:T(8,128)S(1)}, f32[18,32,8,127]{3,1,2,0:T(8,128)}, u32[]{:S(2)}) copy-start(f32[18,32,8,127]{3,1,2,0:T(8,128)} %copy.77) | copy-start | bytes 7022596
  48.9 5.1 %collective-permute-start.2 = (f32[18,32,1,128]{3,1,2,0:T(8,128)S(1)}, f32[18,32,1,128]{3,1,2,0:T(8,128)S(1)}, u32[]{:S(2)}, u32[]{:S(2)}) collective-permute-start(f32[18,32,1,128]{3,1,2,0:T(8,128)S(1)} %fusion.49), channel_id=1, source_target_pairs={{0,1},{1,2},{2,3},{3,4},{4,5},{5,6},{6,7},{7,8},{8,9},{9,10},{10,1... | collective-permute-start | bytes 884744 | tf_op jit(solution)/shard_map/ppermute | solution.py:17
  49.5 6.6 %collective-permute-start.3 = (f32[18,32,1,128]{3,1,2,0:T(8,128)S(1)}, f32[18,32,1,128]{3,1,2,0:T(8,128)S(1)}, u32[]{:S(2)}, u32[]{:S(2)}) collective-permute-start(f32[18,32,1,128]{3,1,2,0:T(8,128)S(1)} %slice.251), channel_id=1, source_target_pairs={{0,63},{1,0},{2,1},{3,2},{4,3},{5,4},{6,5},{7,6},{8,7},{9,8},{10,9... | collective-permute-start | bytes 884744 | tf_op jit(solution)/shard_map/ppermute | solution.py:17
  61.2 7.4 %collective-permute-start.4 = (f32[18,32,1,128]{3,1,2,0:T(8,128)S(1)}, f32[18,32,1,128]{3,1,2,0:T(8,128)S(1)}, u32[]{:S(2)}, u32[]{:S(2)}) collective-permute-start(f32[18,32,1,128]{3,1,2,0:T(8,128)S(1)} %fusion.48), channel_id=1, source_target_pairs={{0,1},{1,2},{2,3},{3,4},{4,5},{5,6},{6,7},{7,8},{8,9},{9,10},{10,1... | collective-permute-start | bytes 884744 | tf_op jit(solution)/shard_map/ppermute | solution.py:17
  62.9 8.1 %collective-permute-start.5 = (f32[18,32,1,128]{3,1,2,0:T(8,128)S(1)}, f32[18,32,1,128]{3,1,2,0:T(8,128)S(1)}, u32[]{:S(2)}, u32[]{:S(2)}) collective-permute-start(f32[18,32,1,128]{3,1,2,0:T(8,128)S(1)} %slice.268), channel_id=1, source_target_pairs={{0,63},{1,0},{2,1},{3,2},{4,3},{5,4},{6,5},{7,6},{8,7},{9,8},{10,9... | collective-permute-start | bytes 884744 | tf_op jit(solution)/shard_map/ppermute | solution.py:17
  75.0 2.4 %copy-start = (f32[36,32,8,128]{3,1,2,0:T(8,128)}, f32[36,32,8,128]{3,1,2,0:T(8,128)S(1)}, u32[]{:S(2)}) copy-start(f32[36,32,8,128]{3,1,2,0:T(8,128)S(1)} %get-tuple-element.9) | copy-start | bytes 14155780
  92.7 32.1 %all-to-all-start.1 = ((f32[32,1,128]{2,1,0:T(1,128)}), f32[32,1,128]{2,1,0:T(1,128)S(1)}, u32[]{:S(2)}, u32[]{:S(2)}) async-start(f32[32,1,128]{2,1,0:T(1,128)} %reshape.295), calls=%async_computation.1 | async-start | bytes 32768 | tf_op jit(solution)/shard_map/all_to_all | solution.py:35
where the time goes:
time: 127 us
  starting transfers between devices  43.2 us (34%)
  local copies, waits for them, and re-layouts  33.2 us (26%)
  other arithmetic  23.8 us (19%)
  waiting for transfers between devices  11.5 us (9%)
  blocking collectives  9.05 us (7%)
  matrix products  4.8 us (4%)
    ppermute x6, starting transfers between devices, passed_along(): return lax.ppermute(value, axis, pairs)  31.4 us
    unnamed x25, local copies, waits for them, and re-layouts  16.7 us
    add x6, other arithmetic, upwind(): center - jnp.maximum(along_x, 0.0) * (center - west_cell)  13.5 us
    all_to_all x1, starting transfers between devices, moved_by_axis(): out = lax.all_to_all(out, axes[k], k, k, tiled=True)  11.8 us
    all_to_all x1, waiting for transfers between devices, moved_by_axis(): out = lax.all_to_all(out, axes[k], k, k, tiled=True)  11.4 us
    all_to_all x1, blocking collectives, moved_by_axis(): out = lax.all_to_all(out, axes[k], k, k, tiled=True)  9.05 us
    slice x4, local copies, waits for them, and re-layouts, upwind(): south_cell = jnp.concatenate([border, center[..., :-1]], axis=3)  5.63 us
    div x2, other arithmetic, sources(): return (advected * (1.0 + growth) / (1.0 + damping), growth * advected)  2.77 us
  transfers between devices with their start and end apart: 7, of which 1 were waited for; matrix products, arithmetic and copies ran while one was open for 26% of the time, Pallas kernels for 0%

commit v1 on v0

v1 whole, which is shorter than its diff:
```python
import functools
import math

import jax
import jax.numpy as jnp
from jax import lax
from jax.experimental import pallas as pl
from jax.experimental.pallas import tpu as pltpu
from jax.sharding import PartitionSpec as P

STEPS = 3
EARLY = 5
MEMBER_GX = ("member", "gx")
MESH = pl.DeviceIdType.MESH


def freq_constants(freqs):
    out = []
    for j in range(freqs):
        shrink = 1.1 ** (-j)
        weight = (j + 1) / freqs
        inverse_speed = 2.0 * math.pi * (0.0418 / shrink) / 9.81
        out.append((0.45 * shrink, 0.05 * inverse_speed, weight, 0.3 * weight * weight))
    return out


def window_kernel(
    sizes,
    spectrum,
    wind,
    land,
    band,
    spectrum_out,
    ocean_out,
    buf,
    grow,
    grow_one,
    wind_v,
    land_v,
    band_v,
    trig,
    send_e,
    send_w,
    recv_e,
    recv_w,
    halo,
    damp,
    damp_edge,
    edge_send,
    edge_recv,
    stokes_c,
    stokes_s,
    place,
    turned,
    fields,
    message,
    arrived,
    load_sem,
    small_sem,
    store_sem,
    halo_send_sem,
    halo_recv_sem,
    edge_send_sem,
    edge_recv_sem,
    message_send_sem,
    message_recv_sem,
    known_sem,
):
    devices, quarter, freqs, lons, lats = sizes
    consts = freq_constants(freqs)
    me = lax.axis_index("gx")
    east = lax.rem(me + 1, devices)
    west = lax.rem(me + devices - 1, devices)

    def load(k):
        return pltpu.make_async_copy(spectrum.at[:, k], buf.at[:, k], load_sem.at[k])

    for k in range(quarter):
        load(k).start()
    small = [
        pltpu.make_async_copy(wind, wind_v, small_sem.at[0]),
        pltpu.make_async_copy(land, land_v, small_sem.at[1]),
        pltpu.make_async_copy(band, band_v, small_sem.at[2]),
    ]
    for copy in small:
        copy.start()

    barrier = pltpu.get_barrier_semaphore()
    for neighbour in (west, east):
        pl.semaphore_signal(barrier, inc=1, device_id={"gx": neighbour}, device_id_type=MESH)

    for k in range(quarter):
        angle = (k + 0.5) * 2.0 * math.pi / (4 * quarter)
        trig[k] = jnp.float32(math.cos(angle))
        trig[quarter + k] = jnp.float32(math.sin(angle))
    rows = lax.broadcasted_iota(jnp.int32, (lons, lats), 0)
    lanes = lax.broadcasted_iota(jnp.int32, (lons, lats), 1)
    first_row = rows == 0
    last_row = rows == lons - 1
    inner_south = jnp.where(lanes == 0, 0.0, 1.0)
    inner_north = jnp.where(lanes == lats - 1, 0.0, 1.0)
    stokes_c[...] = jnp.zeros_like(stokes_c)
    stokes_s[...] = jnp.zeros_like(stokes_s)
    turned[...] = jnp.zeros_like(turned)

    for copy in small:
        copy.wait()
    mask = land_v[...].astype(jnp.float32)
    wind_east = wind_v[0]
    wind_north = wind_v[1]

    pl.semaphore_wait(barrier, 2)

    def tell(n):
        reach = 2**n
        for other in (lax.rem(me + reach, devices), lax.rem(me + devices - reach, devices)):
            pl.semaphore_signal(known_sem.at[n], inc=1, device_id={"gx": other}, device_id_type=MESH)

    def hear(n):
        pl.semaphore_wait(known_sem.at[n], 2)

    rounds = int(math.log2(devices)) - 1
    tell(0)

    def halo_copy(s, k, to_east):
        src, dst, side, where = (send_e, recv_e, 0, east) if to_east else (send_w, recv_w, 1, west)
        return pltpu.make_async_remote_copy(
            src_ref=src.at[s, k],
            dst_ref=dst.at[s, k],
            send_sem=halo_send_sem.at[s, side, k],
            recv_sem=halo_recv_sem.at[s, side, k],
            device_id={"gx": where},
            device_id_type=MESH,
        )

    def edge_copy(s, to_east):
        side, where = (0, east) if to_east else (1, west)
        return pltpu.make_async_remote_copy(
            src_ref=edge_send.at[s, side],
            dst_ref=edge_recv.at[s, side],
            send_sem=edge_send_sem.at[s, side],
            recv_sem=edge_recv_sem.at[s, side],
            device_id={"gx": where},
            device_id_type=MESH,
        )

    def pack(s, k):
        last = pl.ds(lons - 1, freqs, stride=lons)
        first = pl.ds(0, freqs, stride=lons)
        send_e[s, k, :freqs] = buf[0, k, last]
        send_e[s, k, freqs:] = buf[3, k, last]
        send_w[s, k, :freqs] = buf[1, k, first]
        send_w[s, k, freqs:] = buf[2, k, first]

    def ship(s, k):
        halo_copy(s, k, True).start()
        halo_copy(s, k, False).start()

    @pl.loop(0, quarter)
    def _(k):
        load(k).wait()
        pack(0, k)
        ship(0, k)

    hear(0)
    if rounds > 1:
        tell(1)

    def one_step(s):
        def body(k, carry):
            energy, across, along = carry
            c = jnp.full((lons, lats), trig[k], jnp.float32)
            n = jnp.full((lons, lats), trig[quarter + k], jnp.float32)
            both = c + n
            c_south, n_south = c * inner_south, n * inner_south
            c_north, n_north = c * inner_north, n * inner_north
            halo_copy(s, k, True).wait_recv()
            halo_copy(s, k, False).wait_recv()
            if s > 0:
                from_west = damp_edge[0]
                from_east = damp_edge[1]
                halo[0, :freqs] = recv_e[s, k, :freqs] * from_west
                halo[0, freqs:] = recv_e[s, k, freqs:] * from_west
                halo[1, :freqs] = recv_w[s, k, :freqs] * from_east
                halo[1, freqs:] = recv_w[s, k, freqs:] * from_east
            else:
                blow = wind_east * c + wind_north * n
                cross = wind_north * c - wind_east * n
            sum_across = jnp.zeros((lons, lats), jnp.float32)
            sum_along = jnp.zeros((lons, lats), jnp.float32)
            energy = list(energy)
            for j in range(freqs):
                shrink, speed, weight, _ = consts[j]
                tile = pl.ds(j * lons, lons)
                if s > 0:
                    d = damp[tile]
                if s == 0:
                    ahead = blow * speed
                    aside = cross * speed
                    gains = (ahead - 0.05, aside - 0.05, -0.05 - ahead, -0.05 - aside)
                new, flux = [], []
                for q in range(4):
                    center = buf[q, k, tile]
                    if s > 0:
                        center = center * d
                    eastward = q in (0, 3)
                    southern = q < 2
                    row = j + (freqs if q in (2, 3) else 0)
                    if s > 0:
                        edge = halo[0 if eastward else 1, pl.ds(row, 1)]
                    else:
                        edge = (recv_e if eastward else recv_w)[s, k, pl.ds(row, 1)]
                    if eastward:
                        upwind_x = jnp.where(first_row, edge, pltpu.roll(center, 1, 0))
                    else:
                        upwind_x = jnp.where(last_row, edge, pltpu.roll(center, lons - 1, 0))
                    upwind_y = pltpu.roll(center, 1 if southern else lats - 1, 1)
                    c_in, n_in = (c_south, n_south) if southern else (c_north, n_north)
                    x_rate, y_rate = (c, n_in) if q in (0, 2) else (n, c_in)
                    moved = center - shrink * (both * center - x_rate * upwind_x - y_rate * upwind_y)
                    energy[q] = energy[q] + moved
                    if s == 0:
                        gain = mask * jnp.minimum(jnp.maximum(gains[q], 0.0), 0.2)
                        grow[q, k, tile] = gain
                        gain_one = gain + mask
                        grow_one[q, k, tile] = gain_one
                    else:
                        gain_one = grow_one[q, k, tile]
                    value = moved * gain_one
                    buf[q, k, tile] = value
                    if s == STEPS - 1:
                        new.append(value)
                        flux.append(moved * grow[q, k, tile])
                if s == STEPS - 1:
                    sum_across = sum_across + weight * (flux[0] - flux[2])
                    sum_along = sum_along + weight * (flux[1] - flux[3])
                    d02 = new[0] - new[2]
                    d13 = new[1] - new[3]
                    stokes_c[tile] = stokes_c[tile] + (c * d02 - n * d13)
                    stokes_s[tile] = stokes_s[tile] + (n * d02 + c * d13)
            across = across + (c * sum_across - n * sum_along)
            along = along + (n * sum_across + c * sum_along)
            if s < STEPS - 1:
                pack(s + 1, k)

                @pl.when(k < EARLY)
                def _():
                    ship(s + 1, k)

            return tuple(energy), across, along

        zero = jnp.zeros((lons, lats), jnp.float32)
        energy, across, along = lax.fori_loop(0, quarter, body, ((zero,) * 4, zero, zero))
        total = (energy[0] + energy[1]) + (energy[2] + energy[3])
        return mask * total * (1.0 / (4 * quarter * freqs)), across, along

    def set_damping(energy):
        ratio = energy / (0.5 + energy)
        for j in range(freqs):
            damp[pl.ds(j * lons, lons)] = 1.0 / (1.0 + consts[j][3] * ratio)

    edge_weight = (lax.broadcasted_iota(jnp.int32, (freqs, lats), 0).astype(jnp.float32) + 1.0) / freqs
    edge_weight = 0.3 * edge_weight * edge_weight

    for s in range(STEPS):
        energy, across, along = one_step(s)
        if s < STEPS - 1:
            edge_send[s, 0] = energy[lons - 1 :]
            edge_send[s, 1] = energy[:1]
            edge_copy(s, True).start()
            edge_copy(s, False).start()
            for k in range(EARLY, quarter):
                ship(s + 1, k)
        set_damping(energy)
        if s == 0:
            for n in range(1, min(3, rounds)):
                hear(n)
                if n + 1 < rounds:
                    tell(n + 1)
            lat = lax.broadcasted_iota(jnp.int32, (lats, lats), 0)
            place[...] = jnp.where(band_v[...] == lat, 1.0, 0.0).T
        if s == 1 and rounds > 3:
            hear(3)
            if rounds > 4:
                tell(4)
        if s < STEPS - 1:
            for side, to_east in ((0, True), (1, False)):
                edge_copy(s, to_east).wait_recv()
                other = edge_recv[s, side]
                ratio = other / (0.5 + other)
                damp_edge[side] = 1.0 / (1.0 + edge_weight * ratio)

    factor = 3.0 / math.sqrt(4 * quarter * freqs)
    drift_c = jnp.zeros((lons, lats), jnp.float32)
    drift_s = jnp.zeros((lons, lats), jnp.float32)
    for j in range(freqs):
        tile = pl.ds(j * lons, lons)
        d = damp[tile] * consts[j][2]
        drift_c = drift_c + d * stokes_c[tile]
        drift_s = drift_s + d * stokes_s[tile]
    parts = 4 * lons
    for c, value in enumerate((across, along, drift_c, drift_s)):
        value = factor * value
        turned[pl.ds(c * lons, lons), :lats] = value
        turned[pl.ds(parts + c * lons, lons), lats:] = value
    pick = jnp.concatenate(
        [place[pl.ds(0, devices, stride=2)], place[pl.ds(1, devices, stride=2)]], axis=1
    )
    message[:, 0, :] = lax.dot_general(
        pick,
        turned[...],
        (((1,), (1,)), ((), ())),
        precision=lax.Precision.HIGHEST,
        preferred_element_type=jnp.float32,
    )

    if rounds > 4:
        hear(4)

    def message_copy(offset):
        to = lax.rem(me + offset, devices)
        return pltpu.make_async_remote_copy(
            src_ref=message.at[to],
            dst_ref=arrived.at[me],
            send_sem=message_send_sem,
            recv_sem=message_recv_sem,
            device_id={"gx": to},
            device_id_type=MESH,
        )

    half = devices // 2
    message_copy(half).start()

    @pl.loop(1, half)
    def _(near):
        message_copy(half - near).start()
        message_copy(half + near).start()

    arrived[me] = message[me]

    def store(k):
        return pltpu.make_async_copy(buf.at[:, k], spectrum_out.at[:, k], store_sem.at[k])

    @pl.loop(0, quarter)
    def _(k):
        for j in range(freqs):
            tile = pl.ds(j * lons, lons)
            d = damp[tile]
            for q in range(4):
                buf[q, k, tile] = buf[q, k, tile] * d
        store(k).start()

    for s in range(STEPS):
        for k in range(quarter):
            halo_copy(s, k, True).wait_send()
            halo_copy(s, k, False).wait_send()
    for s in range(STEPS - 1):
        edge_copy(s, True).wait_send()
        edge_copy(s, False).wait_send()
    all_out = pltpu.make_async_remote_copy(
        src_ref=message.at[pl.ds(0, devices - 1)],
        dst_ref=arrived.at[pl.ds(0, devices - 1)],
        send_sem=message_send_sem,
        recv_sem=message_recv_sem,
        device_id={"gx": east},
        device_id_type=MESH,
    )
    all_out.wait_send()
    for k in range(quarter):
        store(k).wait()
    all_out.wait_recv()

    per = lats // lons
    block = lanes // lons
    for b in range(devices // per):
        pieces = []
        for h in range(per // 8):
            piece = arrived[pl.ds(b * per + h * 8, 8), 0, :]
            pieces.append(pltpu.roll(piece, h * 8 * lons, 1, stride=lons, stride_axis=0))
        for slot in range(8):
            total = jnp.zeros((8, lats), jnp.float32)
            for h, piece in enumerate(pieces):
                total = total + jnp.where(block == (slot + h * 8 + rows) % per, piece, 0.0)
            line = jnp.sum(total, axis=0, keepdims=True)
            if slot:
                line = pltpu.roll(jnp.broadcast_to(line, (8, lats)), lats - slot * lons, 1)[:1]
            r, c = divmod(slot, 4)
            ocean_out[pl.ds(c * 2 + r, 1), pl.ds(b * lats, lats)] = line


def solution(mesh):
    devices = mesh.shape["gx"]

    def per_device(spectrum, wind, land_sea, band_rows):
        dirs, freqs, lons, lats = spectrum.shape
        quarter = dirs // 4
        tiles = freqs * lons
        f32 = jnp.float32
        any_space = pl.BlockSpec(memory_space=pl.ANY)
        dma = pltpu.SemaphoreType.DMA
        next_spectrum, ocean = pl.pallas_call(
            functools.partial(window_kernel, (devices, quarter, freqs, lons, lats)),
            out_shape=(
                jax.ShapeDtypeStruct((4, quarter, tiles, lats), f32),
                jax.ShapeDtypeStruct((8, devices * lons), f32),
            ),
            in_specs=[any_space] * 4,
            out_specs=(any_space, pl.BlockSpec(memory_space=pltpu.VMEM)),
            scratch_shapes=[
                pltpu.VMEM((4, quarter, tiles, lats), f32),
                pltpu.VMEM((4, quarter, tiles, lats), f32),
                pltpu.VMEM((4, quarter, tiles, lats), f32),
                pltpu.VMEM((2, lons, lats), f32),
                pltpu.VMEM((lons, lats), jnp.int32),
                pltpu.VMEM((1, lats), jnp.int32),
                pltpu.SMEM((2 * quarter,), f32),
                pltpu.VMEM((STEPS, quarter, 2 * freqs, lats), f32),
                pltpu.VMEM((STEPS, quarter, 2 * freqs, lats), f32),
                pltpu.VMEM((STEPS, quarter, 2 * freqs, lats), f32),
                pltpu.VMEM((STEPS, quarter, 2 * freqs, lats), f32),
                pltpu.VMEM((2, 2 * freqs, lats), f32),
                pltpu.VMEM((tiles, lats), f32),
                pltpu.VMEM((2, freqs, lats), f32),
                pltpu.VMEM((STEPS - 1, 2, 1, lats), f32),
                pltpu.VMEM((STEPS - 1, 2, 1, lats), f32),
                pltpu.VMEM((tiles, lats), f32),
                pltpu.VMEM((tiles, lats), f32),
                pltpu.VMEM((lats, lats), f32),
                pltpu.VMEM((lats, 2 * lats), f32),
                pltpu.VMEM((8, lats), f32),
                pltpu.VMEM((devices, 1, lats), f32),
                pltpu.VMEM((devices, 1, lats), f32),
                dma((quarter,)),
                dma((3,)),
                dma((quarter,)),
                dma((STEPS, 2, quarter)),
                dma((STEPS, 2, quarter)),
                dma((STEPS - 1, 2)),
                dma((STEPS - 1, 2)),
                dma,
                dma,
                pltpu.SemaphoreType.REGULAR((5,)),
            ],
            compiler_params=pltpu.CompilerParams(collective_id=0, has_side_effects=True),
        )(
            spectrum.reshape(4, quarter, tiles, lats),
            wind,
            land_sea,
            band_rows.reshape(1, lats),
        )
        ocean = ocean.reshape(4, 2, devices * lons)
        return next_spectrum.reshape(spectrum.shape), ocean

    return jax.shard_map(
        per_device,
        mesh=mesh,
        in_specs=(P(None, None, MEMBER_GX, None), P(None, MEMBER_GX, None), P("gx", None), P(None)),
        out_specs=(P(None, None, MEMBER_GX, None), P(None, "gx", "member")),
        check_vma=False,
    )
```

time: 127 us -> 61.9 us (0.49)
  Pallas kernels: 0 us -> 54.7 us
  starting transfers between devices: 43.2 us -> 0 us
  local copies, waits for them, and re-layouts: 33.2 us -> 6.36 us
  other arithmetic: 23.8 us -> 0 us
  waiting for transfers between devices: 11.5 us -> 0 us
  blocking collectives: 9.05 us -> 0 us
  matrix products: 4.8 us -> 0 us
    pallas_call x0 -> x1, Pallas kernels: none -> 54.7 us  [per_device(): pl.pallas_call(functools.partial(window_kernel, (devices, quarter, freqs,...]
    ppermute x6 -> x0, starting transfers between devices: 31.4 us -> none  [passed_along(): return lax.ppermute(value, axis, pairs)]
    add x10 -> x0, other arithmetic: 13.9 us -> none  [the longest x6 13.5 us: upwind(): center - jnp.maximum(along_x, 0.0) * (center - west_cell)]
    slice x22 -> x0, local copies, waits for them, and re-layouts: 13.4 us -> none  [the longest x4 5.63 us: upwind(): south_cell = jnp.concatenate([border, center[..., :-1]], axis=3)]
    all_to_all x1 -> x0, starting transfers between devices: 11.8 us -> none  [moved_by_axis(): out = lax.all_to_all(out, axes[k], k, k, tiled=True)]
    unnamed x25 -> x1, local copies, waits for them, and re-layouts: 16.7 us -> 5.03 us
    all_to_all x1 -> x0, waiting for transfers between devices: 11.4 us -> none  [moved_by_axis(): out = lax.all_to_all(out, axes[k], k, k, tiled=True)]
    all_to_all x1 -> x0, blocking collectives: 9.05 us -> none  [moved_by_axis(): out = lax.all_to_all(out, axes[k], k, k, tiled=True)]
  transfers between devices with their start and end apart: 7 -> 0, of which waited for: 1 -> 0; matrix products, arithmetic and copies ran while one was open for 26% -> 0% of each run, Pallas kernels for 0% -> 0%
where the time goes in v1:
time: 61.9 us; the launch traced here: 61.7 us
  Pallas kernels  54.7 us (88%)
  local copies, waits for them, and re-layouts  6.36 us (10%)
  between operations  0.64 us (1%)
    pallas_call x1, Pallas kernels, per_device(): pl.pallas_call(functools.partial(window_kernel, (devices, quarter, freqs,...  54.7 us
    unnamed x1, local copies, waits for them, and re-layouts  5.03 us
    reshape x1, local copies, waits for them, and re-layouts, per_device(): ocean = ocean.reshape(4, 2, devices * lons)  1.34 us

profile of v1, /device:TPU:37, one launch (start us, length us, event | category | flops | bytes accessed | tf_op | source)
XLA Modules:
  0.0 61.7 jit_solution(16600557682827862475)
XLA Ops:
  0.6 54.7 %shard_map.59 = (f32[4,9,256,128]{3,2,1,0:T(8,128)}, f32[8,512]{1,0:T(8,128)}) custom-call(f32[4,9,256,128]{3,2,1,0:T(8,128)} %bitcast.3, f32[2,8,128]{2,1,0:T(8,128)} %wind.1, s32[8,128]{1,0:T(8,128)} %land.1, s32[1,128]{1,0:T(1,128)} %bitcast.5), custom_call_target="tpu_custom_call" | custom-call | tf_op jit(solution)/shard_map/pallas_call | solution.py:401
  55.4 1.3 %reshape.19 = f32[4,2,512]{2,1,0:T(2,128)} reshape(f32[8,512]{1,0:T(8,128)} %get-tuple-element.5) | data formatting | bytes 32768 | tf_op jit(solution)/shard_map/reshape | solution.py:451
  56.7 5.0 %copy.7 = f32[36,32,8,128]{3,2,1,0:T(8,128)} copy(f32[36,32,8,128]{3,2,1,0:T(8,128)} %bitcast.4) | data formatting | bytes 9437184

commit v2 on v1

--- a/solution.py
+++ b/solution.py
@@ -10,6 +10,8 @@
 
 STEPS = 3
 EARLY = 5
+KERNEL_VMEM = 36 * 2**20
+HEARD = ((0, 0), (0, 1), (0, 5), (1, 1))
 MEMBER_GX = ("member", "gx")
 MESH = pl.DeviceIdType.MESH
 
@@ -30,9 +32,8 @@
     wind,
     land,
     band,
-    spectrum_out,
-    ocean_out,
     buf,
+    arrived,
     grow,
     grow_one,
     wind_v,
@@ -52,12 +53,9 @@
     stokes_s,
     place,
     turned,
-    fields,
     message,
-    arrived,
     load_sem,
     small_sem,
-    store_sem,
     halo_send_sem,
     halo_recv_sem,
     edge_send_sem,
@@ -162,10 +160,6 @@
         pack(0, k)
         ship(0, k)
 
-    hear(0)
-    if rounds > 1:
-        tell(1)
-
     def one_step(s):
         def body(k, carry):
             energy, across, along = carry
@@ -176,6 +170,14 @@
             c_north, n_north = c * inner_north, n * inner_north
             halo_copy(s, k, True).wait_recv()
             halo_copy(s, k, False).wait_recv()
+            for heard, (at_step, at) in enumerate(HEARD):
+                if at_step == s and heard + 1 < rounds:
+
+                    @pl.when(k == at)
+                    def _(heard=heard):
+                        hear(heard)
+                        tell(heard + 1)
+
             if s > 0:
                 from_west = damp_edge[0]
                 from_east = damp_edge[1]
@@ -273,16 +275,8 @@
                 ship(s + 1, k)
         set_damping(energy)
         if s == 0:
-            for n in range(1, min(3, rounds)):
-                hear(n)
-                if n + 1 < rounds:
-                    tell(n + 1)
             lat = lax.broadcasted_iota(jnp.int32, (lats, lats), 0)
             place[...] = jnp.where(band_v[...] == lat, 1.0, 0.0).T
-        if s == 1 and rounds > 3:
-            hear(3)
-            if rounds > 4:
-                tell(4)
         if s < STEPS - 1:
             for side, to_east in ((0, True), (1, False)):
                 edge_copy(s, to_east).wait_recv()
@@ -314,8 +308,7 @@
         preferred_element_type=jnp.float32,
     )
 
-    if rounds > 4:
-        hear(4)
+    hear(rounds - 1)
 
     def message_copy(offset):
         to = lax.rem(me + offset, devices)
@@ -338,9 +331,6 @@
 
     arrived[me] = message[me]
 
-    def store(k):
-        return pltpu.make_async_copy(buf.at[:, k], spectrum_out.at[:, k], store_sem.at[k])
-
     @pl.loop(0, quarter)
     def _(k):
         for j in range(freqs):
@@ -348,7 +338,6 @@
             d = damp[tile]
             for q in range(4):
                 buf[q, k, tile] = buf[q, k, tile] * d
-        store(k).start()
 
     for s in range(STEPS):
         for k in range(quarter):
@@ -366,12 +355,21 @@
         device_id_type=MESH,
     )
     all_out.wait_send()
-    for k in range(quarter):
-        store(k).wait()
     all_out.wait_recv()
 
+
+def output_kernel(sizes, spectrum, arrived, spectrum_out, ocean_out, ocean, store_sem, ocean_sem):
+    devices, lons, lats = sizes
+    stores = [
+        pltpu.make_async_copy(spectrum.at[q], spectrum_out.at[q], store_sem.at[q]) for q in range(4)
+    ]
+    for copy in stores:
+        copy.start()
+    rows = lax.broadcasted_iota(jnp.int32, (8, lats), 0)
+    block = lax.broadcasted_iota(jnp.int32, (8, lats), 1) // lons
     per = lats // lons
-    block = lanes // lons
+    ahead = lax.rem(block - rows + per, per)
+    wanted = [ahead == n for n in range(per)]
     for b in range(devices // per):
         pieces = []
         for h in range(per // 8):
@@ -380,12 +378,17 @@
         for slot in range(8):
             total = jnp.zeros((8, lats), jnp.float32)
             for h, piece in enumerate(pieces):
-                total = total + jnp.where(block == (slot + h * 8 + rows) % per, piece, 0.0)
+                total = total + jnp.where(wanted[(slot + h * 8) % per], piece, 0.0)
             line = jnp.sum(total, axis=0, keepdims=True)
             if slot:
                 line = pltpu.roll(jnp.broadcast_to(line, (8, lats)), lats - slot * lons, 1)[:1]
             r, c = divmod(slot, 4)
-            ocean_out[pl.ds(c * 2 + r, 1), pl.ds(b * lats, lats)] = line
+            ocean[c, pl.ds(r, 1), pl.ds(b * lats, lats)] = line
+    last = pltpu.make_async_copy(ocean, ocean_out, ocean_sem)
+    last.start()
+    last.wait()
+    for copy in stores:
+        copy.wait()
 
 
 def solution(mesh):
@@ -396,18 +399,18 @@
         quarter = dirs // 4
         tiles = freqs * lons
         f32 = jnp.float32
-        any_space = pl.BlockSpec(memory_space=pl.ANY)
+        hbm_space = pl.BlockSpec(memory_space=pltpu.HBM)
+        vmem_space = pl.BlockSpec(memory_space=pltpu.VMEM)
         dma = pltpu.SemaphoreType.DMA
-        next_spectrum, ocean = pl.pallas_call(
+        final, arrived = pl.pallas_call(
             functools.partial(window_kernel, (devices, quarter, freqs, lons, lats)),
             out_shape=(
-                jax.ShapeDtypeStruct((4, quarter, tiles, lats), f32),
-                jax.ShapeDtypeStruct((8, devices * lons), f32),
+                pltpu.VMEM((4, quarter, tiles, lats), f32),
+                pltpu.VMEM((devices, 1, lats), f32),
             ),
-            in_specs=[any_space] * 4,
-            out_specs=(any_space, pl.BlockSpec(memory_space=pltpu.VMEM)),
+            in_specs=[hbm_space] * 4,
+            out_specs=(vmem_space, vmem_space),
             scratch_shapes=[
-                pltpu.VMEM((4, quarter, tiles, lats), f32),
                 pltpu.VMEM((4, quarter, tiles, lats), f32),
                 pltpu.VMEM((4, quarter, tiles, lats), f32),
                 pltpu.VMEM((2, lons, lats), f32),
@@ -427,12 +430,9 @@
                 pltpu.VMEM((tiles, lats), f32),
                 pltpu.VMEM((lats, lats), f32),
                 pltpu.VMEM((lats, 2 * lats), f32),
-                pltpu.VMEM((8, lats), f32),
-                pltpu.VMEM((devices, 1, lats), f32),
                 pltpu.VMEM((devices, 1, lats), f32),
                 dma((quarter,)),
                 dma((3,)),
-                dma((quarter,)),
                 dma((STEPS, 2, quarter)),
                 dma((STEPS, 2, quarter)),
                 dma((STEPS - 1, 2)),
@@ -441,14 +441,35 @@
                 dma,
                 pltpu.SemaphoreType.REGULAR((5,)),
             ],
-            compiler_params=pltpu.CompilerParams(collective_id=0, has_side_effects=True),
+            compiler_params=pltpu.CompilerParams(
+                collective_id=0, has_side_effects=True, vmem_limit_bytes=KERNEL_VMEM
+            ),
         )(
-            spectrum.reshape(4, quarter, tiles, lats),
-            wind,
-            land_sea,
-            band_rows.reshape(1, lats),
+            *(
+                pltpu.with_memory_space_constraint(argument, pltpu.HBM)
+                for argument in (
+                    spectrum.reshape(4, quarter, tiles, lats),
+                    wind,
+                    land_sea,
+                    band_rows.reshape(1, lats),
+                )
+            )
         )
-        ocean = ocean.reshape(4, 2, devices * lons)
+        next_spectrum, ocean = pl.pallas_call(
+            functools.partial(output_kernel, (devices, lons, lats)),
+            out_shape=(
+                jax.ShapeDtypeStruct((4, quarter, tiles, lats), f32),
+                jax.ShapeDtypeStruct((4, 2, devices * lons), f32),
+            ),
+            in_specs=[vmem_space] * 2,
+            out_specs=(hbm_space, hbm_space),
+            scratch_shapes=[
+                pltpu.VMEM((4, 2, devices * lons), f32),
+                dma((4,)),
+                dma,
+            ],
+            compiler_params=pltpu.CompilerParams(vmem_limit_bytes=KERNEL_VMEM),
+        )(final, arrived)
         return next_spectrum.reshape(spectrum.shape), ocean
 
     return jax.shard_map(

time: 61.9 us -> 57.4 us (0.927)
  local copies, waits for them, and re-layouts: 6.36 us -> 0 us
  Pallas kernels: 54.7 us -> 56.7 us
    unnamed x1 -> x0, local copies, waits for them, and re-layouts: 5.03 us -> none
    pallas_call x0 -> x1, Pallas kernels: none -> 2.23 us  [per_device(): pl.pallas_call(functools.partial(output_kernel, (devices, lons, lats)), o...]
    reshape x1 -> x0, local copies, waits for them, and re-layouts: 1.34 us -> none  [per_device(): ocean = ocean.reshape(4, 2, devices * lons)]
where the time goes in v2:
time: 57.4 us; the launch traced here: 57.3 us
  Pallas kernels  56.7 us (99%)
  between operations  0.64 us (1%)
    pallas_call x1, Pallas kernels, per_device(): pl.pallas_call(functools.partial(window_kernel, (devices, quarter, freqs,...  54.4 us
    pallas_call x1, Pallas kernels, per_device(): pl.pallas_call(functools.partial(output_kernel, (devices, lons, lats)), o...  2.23 us

profile of v2, /device:TPU:37, one launch (start us, length us, event | category | flops | bytes accessed | tf_op | source)
XLA Modules:
  0.0 57.3 jit_solution(4542167902891105661)
XLA Ops:
  0.6 54.4 %shard_map.59 = (f32[4,9,256,128]{3,2,1,0:T(8,128)S(1)}, f32[64,1,128]{2,1,0:T(1,128)S(1)}) custom-call(f32[4,9,256,128]{3,2,1,0:T(8,128)} %bitcast.3, f32[2,8,128]{2,1,0:T(8,128)} %wind.1, s32[8,128]{1,0:T(8,128)} %land.1, s32[1,128]{1,0:T(1,128)} %bitcast.4), custom_call_target="tpu_custom_call" | custom-call | tf_op jit(solution)/shard_map/pallas_call | solution.py:405
  55.1 2.2 %shard_map.60 = (f32[4,9,256,128]{3,2,1,0:T(8,128)}, f32[4,2,512]{2,1,0:T(2,128)}) custom-call(f32[4,9,256,128]{3,2,1,0:T(8,128)S(1)} %get-tuple-element.6.spectrum, f32[64,1,128]{2,1,0:T(1,128)S(1)} %get-tuple-element.7.arrived), custom_call_target="tpu_custom_call" | custom-call | tf_op jit(solution)/shard_map/pallas_call | solution.py:458

commit v3 on v2

--- a/solution.py
+++ b/solution.py
@@ -9,9 +9,10 @@
 from jax.sharding import PartitionSpec as P
 
 STEPS = 3
-EARLY = 5
+EARLY = (5, 4)
+AHEAD = (5, 6, 6)
 KERNEL_VMEM = 36 * 2**20
-HEARD = ((0, 0), (0, 1), (0, 5), (1, 1))
+HEARD = ((-1, 0), (-1, 0), (0, 6), (1, 1))
 MEMBER_GX = ("member", "gx")
 MESH = pl.DeviceIdType.MESH
 
@@ -47,6 +48,7 @@
     halo,
     damp,
     damp_edge,
+    shrink_rows,
     edge_send,
     edge_recv,
     stokes_c,
@@ -93,21 +95,26 @@
         trig[quarter + k] = jnp.float32(math.sin(angle))
     rows = lax.broadcasted_iota(jnp.int32, (lons, lats), 0)
     lanes = lax.broadcasted_iota(jnp.int32, (lons, lats), 1)
-    first_row = rows == 0
-    last_row = rows == lons - 1
+    first_row = jnp.where(rows == 0, 1.0, 0.0)
+    last_row = jnp.where(rows == lons - 1, 1.0, 0.0)
     inner_south = jnp.where(lanes == 0, 0.0, 1.0)
     inner_north = jnp.where(lanes == lats - 1, 0.0, 1.0)
     stokes_c[...] = jnp.zeros_like(stokes_c)
     stokes_s[...] = jnp.zeros_like(stokes_s)
     turned[...] = jnp.zeros_like(turned)
-
-    for copy in small:
-        copy.wait()
-    mask = land_v[...].astype(jnp.float32)
-    wind_east = wind_v[0]
-    wind_north = wind_v[1]
-
-    pl.semaphore_wait(barrier, 2)
+    for j in range(freqs):
+        line = jnp.full((1, lats), consts[j][0], jnp.float32)
+        for rows_of in (shrink_rows, damp_edge.at[0], damp_edge.at[1]):
+            rows_of[pl.ds(j, 1)] = line
+
+    with jax.named_scope("barrier_wait"):
+        for copy in small:
+            copy.wait()
+        mask = land_v[...].astype(jnp.float32)
+        wind_east = wind_v[0]
+        wind_north = wind_v[1]
+
+        pl.semaphore_wait(barrier, 2)
 
     def tell(n):
         reach = 2**n
@@ -154,20 +161,22 @@
         halo_copy(s, k, True).start()
         halo_copy(s, k, False).start()
 
-    @pl.loop(0, quarter)
-    def _(k):
-        load(k).wait()
-        pack(0, k)
-        ship(0, k)
-
-    def one_step(s):
-        def body(k, carry):
-            energy, across, along = carry
-            c = jnp.full((lons, lats), trig[k], jnp.float32)
-            n = jnp.full((lons, lats), trig[quarter + k], jnp.float32)
-            both = c + n
-            c_south, n_south = c * inner_south, n * inner_south
-            c_north, n_north = c * inner_north, n * inner_north
+    with jax.named_scope("first_ship"):
+        @pl.loop(0, quarter)
+        def _(k):
+            load(k).wait()
+            pack(0, k)
+            ship(0, k)
+
+    def body(s, mode, k, carry):
+        energy, across, along = carry
+        c = jnp.full((lons, lats), trig[k], jnp.float32)
+        n = jnp.full((lons, lats), trig[quarter + k], jnp.float32)
+        both = c + n
+        y_rates = ((n * inner_south, c * inner_south), (n * inner_north, c * inner_north))
+        x_rates = (c, n, c, n)
+        sides = (0, 1, 1, 0)
+        if mode != "start":
             halo_copy(s, k, True).wait_recv()
             halo_copy(s, k, False).wait_recv()
             for heard, (at_step, at) in enumerate(HEARD):
@@ -178,81 +187,89 @@
                         hear(heard)
                         tell(heard + 1)
 
-            if s > 0:
-                from_west = damp_edge[0]
-                from_east = damp_edge[1]
-                halo[0, :freqs] = recv_e[s, k, :freqs] * from_west
-                halo[0, freqs:] = recv_e[s, k, freqs:] * from_west
-                halo[1, :freqs] = recv_w[s, k, :freqs] * from_east
-                halo[1, freqs:] = recv_w[s, k, freqs:] * from_east
-            else:
+            for side, got in ((0, recv_e), (1, recv_w)):
+                scale = damp_edge[side]
+                halo[side, :freqs] = got[s, k, :freqs] * scale
+                halo[side, freqs:] = got[s, k, freqs:] * scale
+            outer = [x_rates[q] * (first_row, last_row)[sides[q]] for q in range(4)]
+        if mode != "finish":
+            inner = [x_rates[q] * (1.0 - (first_row, last_row)[sides[q]]) for q in range(4)]
+            if s == 0:
                 blow = wind_east * c + wind_north * n
                 cross = wind_north * c - wind_east * n
-            sum_across = jnp.zeros((lons, lats), jnp.float32)
-            sum_along = jnp.zeros((lons, lats), jnp.float32)
-            energy = list(energy)
-            for j in range(freqs):
-                shrink, speed, weight, _ = consts[j]
-                tile = pl.ds(j * lons, lons)
+        sum_across = jnp.zeros((lons, lats), jnp.float32)
+        sum_along = jnp.zeros((lons, lats), jnp.float32)
+        energy = list(energy)
+        for j in range(freqs):
+            shrink, speed, weight, _ = consts[j]
+            tile = pl.ds(j * lons, lons)
+            if mode != "finish":
                 if s > 0:
                     d = damp[tile]
-                if s == 0:
+                else:
                     ahead = blow * speed
                     aside = cross * speed
                     gains = (ahead - 0.05, aside - 0.05, -0.05 - ahead, -0.05 - aside)
-                new, flux = [], []
-                for q in range(4):
+            new, flux = [], []
+            for q in range(4):
+                if mode == "finish":
+                    moved = buf[q, k, tile]
+                else:
                     center = buf[q, k, tile]
                     if s > 0:
                         center = center * d
-                    eastward = q in (0, 3)
-                    southern = q < 2
-                    row = j + (freqs if q in (2, 3) else 0)
-                    if s > 0:
-                        edge = halo[0 if eastward else 1, pl.ds(row, 1)]
-                    else:
-                        edge = (recv_e if eastward else recv_w)[s, k, pl.ds(row, 1)]
-                    if eastward:
-                        upwind_x = jnp.where(first_row, edge, pltpu.roll(center, 1, 0))
-                    else:
-                        upwind_x = jnp.where(last_row, edge, pltpu.roll(center, lons - 1, 0))
-                    upwind_y = pltpu.roll(center, 1 if southern else lats - 1, 1)
-                    c_in, n_in = (c_south, n_south) if southern else (c_north, n_north)
-                    x_rate, y_rate = (c, n_in) if q in (0, 2) else (n, c_in)
-                    moved = center - shrink * (both * center - x_rate * upwind_x - y_rate * upwind_y)
-                    energy[q] = energy[q] + moved
+                    upwind_x = pltpu.roll(center, lons - 1 if sides[q] else 1, 0)
+                    upwind_y = pltpu.roll(center, 1 if q < 2 else lats - 1, 1)
+                    change = both * center - inner[q] * upwind_x - y_rates[q // 2][q % 2] * upwind_y
+                    moved = center - shrink * change
                     if s == 0:
                         gain = mask * jnp.minimum(jnp.maximum(gains[q], 0.0), 0.2)
                         grow[q, k, tile] = gain
                         gain_one = gain + mask
                         grow_one[q, k, tile] = gain_one
-                    else:
-                        gain_one = grow_one[q, k, tile]
-                    value = moved * gain_one
-                    buf[q, k, tile] = value
-                    if s == STEPS - 1:
-                        new.append(value)
-                        flux.append(moved * grow[q, k, tile])
+                if mode == "start":
+                    buf[q, k, tile] = moved
+                    continue
+                row = j + (freqs if q >= 2 else 0)
+                moved = moved + outer[q] * halo[sides[q], pl.ds(row, 1)]
+                energy[q] = energy[q] + moved
+                if s > 0 or mode == "finish":
+                    gain_one = grow_one[q, k, tile]
+                value = moved * gain_one
+                buf[q, k, tile] = value
                 if s == STEPS - 1:
-                    sum_across = sum_across + weight * (flux[0] - flux[2])
-                    sum_along = sum_along + weight * (flux[1] - flux[3])
-                    d02 = new[0] - new[2]
-                    d13 = new[1] - new[3]
-                    stokes_c[tile] = stokes_c[tile] + (c * d02 - n * d13)
-                    stokes_s[tile] = stokes_s[tile] + (n * d02 + c * d13)
-            across = across + (c * sum_across - n * sum_along)
-            along = along + (n * sum_across + c * sum_along)
-            if s < STEPS - 1:
-                pack(s + 1, k)
-
-                @pl.when(k < EARLY)
-                def _():
-                    ship(s + 1, k)
-
-            return tuple(energy), across, along
-
-        zero = jnp.zeros((lons, lats), jnp.float32)
-        energy, across, along = lax.fori_loop(0, quarter, body, ((zero,) * 4, zero, zero))
+                    new.append(value)
+                    flux.append(moved * grow[q, k, tile])
+            if s == STEPS - 1 and mode != "start":
+                sum_across = sum_across + weight * (flux[0] - flux[2])
+                sum_along = sum_along + weight * (flux[1] - flux[3])
+                d02 = new[0] - new[2]
+                d13 = new[1] - new[3]
+                stokes_c[tile] = stokes_c[tile] + (c * d02 - n * d13)
+                stokes_s[tile] = stokes_s[tile] + (n * d02 + c * d13)
+        if mode == "start":
+            return carry
+        across = across + (c * sum_across - n * sum_along)
+        along = along + (n * sum_across + c * sum_along)
+        if s < STEPS - 1:
+            pack(s + 1, k)
+
+            @pl.when(k < EARLY[s])
+            def _():
+                ship(s + 1, k)
+
+        return tuple(energy), across, along
+
+    zero = jnp.zeros((lons, lats), jnp.float32)
+    nothing = ((zero,) * 4, zero, zero)
+
+    def start_step(s):
+        lax.fori_loop(0, AHEAD[s], functools.partial(body, s, "start"), nothing)
+
+    def finish_step(s):
+        carry = lax.fori_loop(0, AHEAD[s], functools.partial(body, s, "finish"), nothing)
+        carry = lax.fori_loop(AHEAD[s], quarter, functools.partial(body, s, "full"), carry)
+        energy, across, along = carry
         total = (energy[0] + energy[1]) + (energy[2] + energy[3])
         return mask * total * (1.0 / (4 * quarter * freqs)), across, along
 
@@ -261,54 +278,65 @@
         for j in range(freqs):
             damp[pl.ds(j * lons, lons)] = 1.0 / (1.0 + consts[j][3] * ratio)
 
+    with jax.named_scope("start0"):
+        start_step(0)
+    for heard in (0, 1):
+        hear(heard)
+        tell(heard + 1)
     edge_weight = (lax.broadcasted_iota(jnp.int32, (freqs, lats), 0).astype(jnp.float32) + 1.0) / freqs
     edge_weight = 0.3 * edge_weight * edge_weight
 
     for s in range(STEPS):
-        energy, across, along = one_step(s)
+        with jax.named_scope(f"step{s}"):
+            energy, across, along = finish_step(s)
         if s < STEPS - 1:
             edge_send[s, 0] = energy[lons - 1 :]
             edge_send[s, 1] = energy[:1]
             edge_copy(s, True).start()
             edge_copy(s, False).start()
-            for k in range(EARLY, quarter):
+            for k in range(EARLY[s], quarter):
                 ship(s + 1, k)
         set_damping(energy)
         if s == 0:
             lat = lax.broadcasted_iota(jnp.int32, (lats, lats), 0)
             place[...] = jnp.where(band_v[...] == lat, 1.0, 0.0).T
         if s < STEPS - 1:
+            with jax.named_scope(f"start{s + 1}"):
+                start_step(s + 1)
             for side, to_east in ((0, True), (1, False)):
-                edge_copy(s, to_east).wait_recv()
+                with jax.named_scope(f"edge{s}{side}"):
+                    edge_copy(s, to_east).wait_recv()
                 other = edge_recv[s, side]
                 ratio = other / (0.5 + other)
-                damp_edge[side] = 1.0 / (1.0 + edge_weight * ratio)
-
-    factor = 3.0 / math.sqrt(4 * quarter * freqs)
-    drift_c = jnp.zeros((lons, lats), jnp.float32)
-    drift_s = jnp.zeros((lons, lats), jnp.float32)
-    for j in range(freqs):
-        tile = pl.ds(j * lons, lons)
-        d = damp[tile] * consts[j][2]
-        drift_c = drift_c + d * stokes_c[tile]
-        drift_s = drift_s + d * stokes_s[tile]
-    parts = 4 * lons
-    for c, value in enumerate((across, along, drift_c, drift_s)):
-        value = factor * value
-        turned[pl.ds(c * lons, lons), :lats] = value
-        turned[pl.ds(parts + c * lons, lons), lats:] = value
-    pick = jnp.concatenate(
-        [place[pl.ds(0, devices, stride=2)], place[pl.ds(1, devices, stride=2)]], axis=1
-    )
-    message[:, 0, :] = lax.dot_general(
-        pick,
-        turned[...],
-        (((1,), (1,)), ((), ())),
-        precision=lax.Precision.HIGHEST,
-        preferred_element_type=jnp.float32,
-    )
-
-    hear(rounds - 1)
+                damp_edge[side] = shrink_rows[...] / (1.0 + edge_weight * ratio)
+
+    with jax.named_scope("fields"):
+        factor = 3.0 / math.sqrt(4 * quarter * freqs)
+        drift_c = jnp.zeros((lons, lats), jnp.float32)
+        drift_s = jnp.zeros((lons, lats), jnp.float32)
+        for j in range(freqs):
+            tile = pl.ds(j * lons, lons)
+            d = damp[tile] * consts[j][2]
+            drift_c = drift_c + d * stokes_c[tile]
+            drift_s = drift_s + d * stokes_s[tile]
+        parts = 4 * lons
+        for c, value in enumerate((across, along, drift_c, drift_s)):
+            value = factor * value
+            turned[pl.ds(c * lons, lons), :lats] = value
+            turned[pl.ds(parts + c * lons, lons), lats:] = value
+        pick = jnp.concatenate(
+            [place[pl.ds(0, devices, stride=2)], place[pl.ds(1, devices, stride=2)]], axis=1
+        )
+        message[:, 0, :] = lax.dot_general(
+            pick,
+            turned[...],
+            (((1,), (1,)), ((), ())),
+            precision=lax.Precision.HIGHEST,
+            preferred_element_type=jnp.float32,
+        )
+
+    with jax.named_scope("hear"):
+        hear(rounds - 1)
 
     def message_copy(offset):
         to = lax.rem(me + offset, devices)
@@ -321,13 +349,14 @@
             device_id_type=MESH,
         )
 
-    half = devices // 2
-    message_copy(half).start()
-
-    @pl.loop(1, half)
-    def _(near):
-        message_copy(half - near).start()
-        message_copy(half + near).start()
+    with jax.named_scope("issue"):
+        half = devices // 2
+        message_copy(half).start()
+
+        @pl.loop(1, half)
+        def _(near):
+            message_copy(half - near).start()
+            message_copy(half + near).start()
 
     arrived[me] = message[me]
 
@@ -354,8 +383,10 @@
         device_id={"gx": east},
         device_id_type=MESH,
     )
-    all_out.wait_send()
-    all_out.wait_recv()
+    with jax.named_scope("wait_send"):
+        all_out.wait_send()
+    with jax.named_scope("wait_recv"):
+        all_out.wait_recv()
 
 
 def output_kernel(sizes, spectrum, arrived, spectrum_out, ocean_out, ocean, store_sem, ocean_sem):
@@ -424,6 +455,7 @@
                 pltpu.VMEM((2, 2 * freqs, lats), f32),
                 pltpu.VMEM((tiles, lats), f32),
                 pltpu.VMEM((2, freqs, lats), f32),
+                pltpu.VMEM((freqs, lats), f32),
                 pltpu.VMEM((STEPS - 1, 2, 1, lats), f32),
                 pltpu.VMEM((STEPS - 1, 2, 1, lats), f32),
                 pltpu.VMEM((tiles, lats), f32),

time: 57.4 us -> 54.9 us (0.956)
  Pallas kernels: 56.7 us -> 54.2 us
    pallas_call x1, Pallas kernels: 54.4 us -> 52 us  [per_device(): pl.pallas_call(functools.partial(window_kernel, (devices, quarter, freqs,...]
where the time goes in v3:
time: 54.9 us; the launch traced here: 54.8 us
  Pallas kernels  54.2 us (99%)
  between operations  0.64 us (1%)
    pallas_call x1, Pallas kernels, per_device(): pl.pallas_call(functools.partial(window_kernel, (devices, quarter, freqs,...  52 us
    pallas_call x1, Pallas kernels, per_device(): pl.pallas_call(functools.partial(output_kernel, (devices, lons, lats)), o...  2.23 us

profile of v3, /device:TPU:37, one launch (start us, length us, event | category | flops | bytes accessed | tf_op | source)
XLA Modules:
  0.0 54.8 jit_solution(17608135398381818261)
XLA Ops:
  0.6 52.0 %shard_map.59 = (f32[4,9,256,128]{3,2,1,0:T(8,128)S(1)}, f32[64,1,128]{2,1,0:T(1,128)S(1)}) custom-call(f32[4,9,256,128]{3,2,1,0:T(8,128)} %bitcast.3, f32[2,8,128]{2,1,0:T(8,128)} %wind.1, s32[8,128]{1,0:T(8,128)} %land.1, s32[1,128]{1,0:T(1,128)} %bitcast.4), custom_call_target="tpu_custom_call" | custom-call | tf_op jit(solution)/shard_map/pallas_call | solution.py:436
  52.6 2.2 %shard_map.60 = (f32[4,9,256,128]{3,2,1,0:T(8,128)}, f32[4,2,512]{2,1,0:T(2,128)}) custom-call(f32[4,9,256,128]{3,2,1,0:T(8,128)S(1)} %get-tuple-element.6.spectrum, f32[64,1,128]{2,1,0:T(1,128)S(1)} %get-tuple-element.7.arrived), custom_call_target="tpu_custom_call" | custom-call | tf_op jit(solution)/shard_map/pallas_call | solution.py:490

commit v4 on v3

--- a/solution.py
+++ b/solution.py
@@ -9,10 +9,9 @@
 from jax.sharding import PartitionSpec as P
 
 STEPS = 3
-EARLY = (5, 4)
-AHEAD = (5, 6, 6)
+EARLY = (4, 4)
 KERNEL_VMEM = 36 * 2**20
-HEARD = ((-1, 0), (-1, 0), (0, 6), (1, 1))
+HEARD = 7
 MEMBER_GX = ("member", "gx")
 MESH = pl.DeviceIdType.MESH
 
@@ -124,7 +123,8 @@
     def hear(n):
         pl.semaphore_wait(known_sem.at[n], 2)
 
-    rounds = int(math.log2(devices)) - 1
+    rounds = 5
+    assert 2 ** (rounds + 1) == devices
     tell(0)
 
     def halo_copy(s, k, to_east):
@@ -176,23 +176,22 @@
         y_rates = ((n * inner_south, c * inner_south), (n * inner_north, c * inner_north))
         x_rates = (c, n, c, n)
         sides = (0, 1, 1, 0)
-        if mode != "start":
+        if mode == "finish":
             halo_copy(s, k, True).wait_recv()
             halo_copy(s, k, False).wait_recv()
-            for heard, (at_step, at) in enumerate(HEARD):
-                if at_step == s and heard + 1 < rounds:
-
-                    @pl.when(k == at)
-                    def _(heard=heard):
-                        hear(heard)
-                        tell(heard + 1)
+            if s == 0:
+
+                @pl.when(k == HEARD)
+                def _():
+                    hear(2)
+                    tell(3)
 
             for side, got in ((0, recv_e), (1, recv_w)):
                 scale = damp_edge[side]
                 halo[side, :freqs] = got[s, k, :freqs] * scale
                 halo[side, freqs:] = got[s, k, freqs:] * scale
             outer = [x_rates[q] * (first_row, last_row)[sides[q]] for q in range(4)]
-        if mode != "finish":
+        else:
             inner = [x_rates[q] * (1.0 - (first_row, last_row)[sides[q]]) for q in range(4)]
             if s == 0:
                 blow = wind_east * c + wind_north * n
@@ -233,14 +232,12 @@
                 row = j + (freqs if q >= 2 else 0)
                 moved = moved + outer[q] * halo[sides[q], pl.ds(row, 1)]
                 energy[q] = energy[q] + moved
-                if s > 0 or mode == "finish":
-                    gain_one = grow_one[q, k, tile]
-                value = moved * gain_one
+                value = moved * grow_one[q, k, tile]
                 buf[q, k, tile] = value
                 if s == STEPS - 1:
                     new.append(value)
                     flux.append(moved * grow[q, k, tile])
-            if s == STEPS - 1 and mode != "start":
+            if s == STEPS - 1 and mode == "finish":
                 sum_across = sum_across + weight * (flux[0] - flux[2])
                 sum_along = sum_along + weight * (flux[1] - flux[3])
                 d02 = new[0] - new[2]
@@ -264,12 +261,12 @@
     nothing = ((zero,) * 4, zero, zero)
 
     def start_step(s):
-        lax.fori_loop(0, AHEAD[s], functools.partial(body, s, "start"), nothing)
+        lax.fori_loop(0, quarter, functools.partial(body, s, "start"), nothing)
 
     def finish_step(s):
-        carry = lax.fori_loop(0, AHEAD[s], functools.partial(body, s, "finish"), nothing)
-        carry = lax.fori_loop(AHEAD[s], quarter, functools.partial(body, s, "full"), carry)
-        energy, across, along = carry
+        energy, across, along = lax.fori_loop(
+            0, quarter, functools.partial(body, s, "finish"), nothing
+        )
         total = (energy[0] + energy[1]) + (energy[2] + energy[3])
         return mask * total * (1.0 / (4 * quarter * freqs)), across, along
 
@@ -278,11 +275,12 @@
         for j in range(freqs):
             damp[pl.ds(j * lons, lons)] = 1.0 / (1.0 + consts[j][3] * ratio)
 
+    hear(0)
+    tell(1)
     with jax.named_scope("start0"):
         start_step(0)
-    for heard in (0, 1):
-        hear(heard)
-        tell(heard + 1)
+    hear(1)
+    tell(2)
     edge_weight = (lax.broadcasted_iota(jnp.int32, (freqs, lats), 0).astype(jnp.float32) + 1.0) / freqs
     edge_weight = 0.3 * edge_weight * edge_weight
 
@@ -303,6 +301,9 @@
         if s < STEPS - 1:
             with jax.named_scope(f"start{s + 1}"):
                 start_step(s + 1)
+            if s == 0:
+                hear(3)
+                tell(4)
             for side, to_east in ((0, True), (1, False)):
                 with jax.named_scope(f"edge{s}{side}"):
                     edge_copy(s, to_east).wait_recv()

time: 54.9 us -> 54.2 us (0.987)
  Pallas kernels: 54.2 us -> 53.4 us
    pallas_call x1, Pallas kernels: 52 us -> 51.2 us  [per_device(): pl.pallas_call(functools.partial(window_kernel, (devices, quarter, freqs,...]
where the time goes in v4:
time: 54.2 us; the launch traced here: 54.1 us
  Pallas kernels  53.4 us (99%)
  between operations  0.64 us (1%)
    pallas_call x1, Pallas kernels, per_device(): pl.pallas_call(functools.partial(window_kernel, (devices, quarter, freqs,...  51.2 us
    pallas_call x1, Pallas kernels, per_device(): pl.pallas_call(functools.partial(output_kernel, (devices, lons, lats)), o...  2.23 us

profile of v4, /device:TPU:37, one launch (start us, length us, event | category | flops | bytes accessed | tf_op | source)
XLA Modules:
  0.0 54.1 jit_solution(762992629778636748)
XLA Ops:
  0.6 51.2 %shard_map.59 = (f32[4,9,256,128]{3,2,1,0:T(8,128)S(1)}, f32[64,1,128]{2,1,0:T(1,128)S(1)}) custom-call(f32[4,9,256,128]{3,2,1,0:T(8,128)} %bitcast.3, f32[2,8,128]{2,1,0:T(8,128)} %wind.1, s32[8,128]{1,0:T(8,128)} %land.1, s32[1,128]{1,0:T(1,128)} %bitcast.4), custom_call_target="tpu_custom_call" | custom-call | tf_op jit(solution)/shard_map/pallas_call | solution.py:437
  51.8 2.2 %shard_map.60 = (f32[4,9,256,128]{3,2,1,0:T(8,128)}, f32[4,2,512]{2,1,0:T(2,128)}) custom-call(f32[4,9,256,128]{3,2,1,0:T(8,128)S(1)} %get-tuple-element.6.spectrum, f32[64,1,128]{2,1,0:T(1,128)S(1)} %get-tuple-element.7.arrived), custom_call_target="tpu_custom_call" | custom-call | tf_op jit(solution)/shard_map/pallas_call | solution.py:491

commit v5 on v4

--- a/solution.py
+++ b/solution.py
@@ -9,9 +9,9 @@
 from jax.sharding import PartitionSpec as P
 
 STEPS = 3
-EARLY = (4, 4)
+EARLY = (5, 5)
 KERNEL_VMEM = 36 * 2**20
-HEARD = 7
+HEARD = ((0, 3), (0, 9), (0, 6), (1, 2))
 MEMBER_GX = ("member", "gx")
 MESH = pl.DeviceIdType.MESH
 
@@ -71,11 +71,13 @@
     east = lax.rem(me + 1, devices)
     west = lax.rem(me + devices - 1, devices)
 
+    barrier = pltpu.get_barrier_semaphore()
+    for neighbour in (west, east):
+        pl.semaphore_signal(barrier, inc=1, device_id={"gx": neighbour}, device_id_type=MESH)
+
     def load(k):
         return pltpu.make_async_copy(spectrum.at[:, k], buf.at[:, k], load_sem.at[k])
 
-    for k in range(quarter):
-        load(k).start()
     small = [
         pltpu.make_async_copy(wind, wind_v, small_sem.at[0]),
         pltpu.make_async_copy(land, land_v, small_sem.at[1]),
@@ -84,9 +86,8 @@
     for copy in small:
         copy.start()
 
-    barrier = pltpu.get_barrier_semaphore()
-    for neighbour in (west, east):
-        pl.semaphore_signal(barrier, inc=1, device_id={"gx": neighbour}, device_id_type=MESH)
+    for k in range(quarter):
+        load(k).start()
 
     for k in range(quarter):
         angle = (k + 0.5) * 2.0 * math.pi / (4 * quarter)
@@ -107,12 +108,6 @@
             rows_of[pl.ds(j, 1)] = line
 
     with jax.named_scope("barrier_wait"):
-        for copy in small:
-            copy.wait()
-        mask = land_v[...].astype(jnp.float32)
-        wind_east = wind_v[0]
-        wind_north = wind_v[1]
-
         pl.semaphore_wait(barrier, 2)
 
     def tell(n):
@@ -167,6 +162,12 @@
             load(k).wait()
             pack(0, k)
             ship(0, k)
+
+    for copy in small:
+        copy.wait()
+    mask = land_v[...].astype(jnp.float32)
+    wind_east = wind_v[0]
+    wind_north = wind_v[1]
 
     def body(s, mode, k, carry):
         energy, across, along = carry
@@ -179,12 +180,13 @@
         if mode == "finish":
             halo_copy(s, k, True).wait_recv()
             halo_copy(s, k, False).wait_recv()
-            if s == 0:
-
-                @pl.when(k == HEARD)
-                def _():
-                    hear(2)
-                    tell(3)
+            for heard in (2, 3):
+                if HEARD[heard][0] == s:
+
+                    @pl.when(k == HEARD[heard][1])
+                    def _(heard=heard):
+                        hear(heard)
+                        tell(heard + 1)
 
             for side, got in ((0, recv_e), (1, recv_w)):
                 scale = damp_edge[side]
@@ -194,6 +196,12 @@
         else:
             inner = [x_rates[q] * (1.0 - (first_row, last_row)[sides[q]]) for q in range(4)]
             if s == 0:
+
+                @pl.when(k == HEARD[0][1])
+                def _():
+                    hear(0)
+                    tell(1)
+
                 blow = wind_east * c + wind_north * n
                 cross = wind_north * c - wind_east * n
         sum_across = jnp.zeros((lons, lats), jnp.float32)
@@ -275,8 +283,6 @@
         for j in range(freqs):
             damp[pl.ds(j * lons, lons)] = 1.0 / (1.0 + consts[j][3] * ratio)
 
-    hear(0)
-    tell(1)
     with jax.named_scope("start0"):
         start_step(0)
     hear(1)
@@ -301,9 +307,6 @@
         if s < STEPS - 1:
             with jax.named_scope(f"start{s + 1}"):
                 start_step(s + 1)
-            if s == 0:
-                hear(3)
-                tell(4)
             for side, to_east in ((0, True), (1, False)):
                 with jax.named_scope(f"edge{s}{side}"):
                     edge_copy(s, to_east).wait_recv()

time: 54.2 us -> 53.9 us (level)
  no operation moved by 1% of the time
where the time goes in v5:
time: 53.9 us; the launch traced here: 53.8 us
  Pallas kernels  53.1 us (99%)
  between operations  0.64 us (1%)
    pallas_call x1, Pallas kernels, per_device(): pl.pallas_call(functools.partial(window_kernel, (devices, quarter, freqs,...  50.9 us
    pallas_call x1, Pallas kernels, per_device(): pl.pallas_call(functools.partial(output_kernel, (devices, lons, lats)), o...  2.23 us

profile of v5, /device:TPU:37, one launch (start us, length us, event | category | flops | bytes accessed | tf_op | source)
XLA Modules:
  0.0 53.8 jit_solution(8294641606962635838)
XLA Ops:
  0.6 50.9 %shard_map.59 = (f32[4,9,256,128]{3,2,1,0:T(8,128)S(1)}, f32[64,1,128]{2,1,0:T(1,128)S(1)}) custom-call(f32[4,9,256,128]{3,2,1,0:T(8,128)} %bitcast.3, f32[2,8,128]{2,1,0:T(8,128)} %wind.1, s32[8,128]{1,0:T(8,128)} %land.1, s32[1,128]{1,0:T(1,128)} %bitcast.4), custom_call_target="tpu_custom_call" | custom-call | tf_op jit(solution)/shard_map/pallas_call | solution.py:440
  51.5 2.2 %shard_map.60 = (f32[4,9,256,128]{3,2,1,0:T(8,128)}, f32[4,2,512]{2,1,0:T(2,128)}) custom-call(f32[4,9,256,128]{3,2,1,0:T(8,128)S(1)} %get-tuple-element.6.spectrum, f32[64,1,128]{2,1,0:T(1,128)S(1)} %get-tuple-element.7.arrived), custom_call_target="tpu_custom_call" | custom-call | tf_op jit(solution)/shard_map/pallas_call | solution.py:494

commit v6 on v5

--- a/solution.py
+++ b/solution.py
@@ -9,7 +9,7 @@
 from jax.sharding import PartitionSpec as P
 
 STEPS = 3
-EARLY = (5, 5)
+EARLY = (5, 4)
 KERNEL_VMEM = 36 * 2**20
 HEARD = ((0, 3), (0, 9), (0, 6), (1, 2))
 MEMBER_GX = ("member", "gx")

time: 53.9 us -> 53.8 us (level)
  no operation moved by 1% of the time
where the time goes in v6:
time: 53.8 us; the launch traced here: 53.7 us
  Pallas kernels  53.1 us (99%)
  between operations  0.64 us (1%)
    pallas_call x1, Pallas kernels, per_device(): pl.pallas_call(functools.partial(window_kernel, (devices, quarter, freqs,...  50.8 us
    pallas_call x1, Pallas kernels, per_device(): pl.pallas_call(functools.partial(output_kernel, (devices, lons, lats)), o...  2.23 us

profile of v6, /device:TPU:37, one launch (start us, length us, event | category | flops | bytes accessed | tf_op | source)
XLA Modules:
  0.0 53.7 jit_solution(15896020662455848343)
XLA Ops:
  0.6 50.8 %shard_map.59 = (f32[4,9,256,128]{3,2,1,0:T(8,128)S(1)}, f32[64,1,128]{2,1,0:T(1,128)S(1)}) custom-call(f32[4,9,256,128]{3,2,1,0:T(8,128)} %bitcast.3, f32[2,8,128]{2,1,0:T(8,128)} %wind.1, s32[8,128]{1,0:T(8,128)} %land.1, s32[1,128]{1,0:T(1,128)} %bitcast.4), custom_call_target="tpu_custom_call" | custom-call | tf_op jit(solution)/shard_map/pallas_call | solution.py:440
  51.5 2.2 %shard_map.60 = (f32[4,9,256,128]{3,2,1,0:T(8,128)}, f32[4,2,512]{2,1,0:T(2,128)}) custom-call(f32[4,9,256,128]{3,2,1,0:T(8,128)S(1)} %get-tuple-element.6.spectrum, f32[64,1,128]{2,1,0:T(1,128)S(1)} %get-tuple-element.7.arrived), custom_call_target="tpu_custom_call" | custom-call | tf_op jit(solution)/shard_map/pallas_call | solution.py:494

commit v7 on v6

--- a/solution.py
+++ b/solution.py
@@ -337,7 +337,7 @@
             (((1,), (1,)), ((), ())),
             precision=lax.Precision.HIGHEST,
             preferred_element_type=jnp.float32,
-        )
+        )[:, : 2 * parts]
 
     with jax.named_scope("hear"):
         hear(rounds - 1)
@@ -409,6 +409,7 @@
         pieces = []
         for h in range(per // 8):
             piece = arrived[pl.ds(b * per + h * 8, 8), 0, :]
+            piece = jnp.concatenate([piece, jnp.zeros_like(piece)], axis=1)
             pieces.append(pltpu.roll(piece, h * 8 * lons, 1, stride=lons, stride_axis=0))
         for slot in range(8):
             total = jnp.zeros((8, lats), jnp.float32)
@@ -441,7 +442,7 @@
             functools.partial(window_kernel, (devices, quarter, freqs, lons, lats)),
             out_shape=(
                 pltpu.VMEM((4, quarter, tiles, lats), f32),
-                pltpu.VMEM((devices, 1, lats), f32),
+                pltpu.VMEM((devices, 1, 8 * lons), f32),
             ),
             in_specs=[hbm_space] * 4,
             out_specs=(vmem_space, vmem_space),
@@ -466,7 +467,7 @@
                 pltpu.VMEM((tiles, lats), f32),
                 pltpu.VMEM((lats, lats), f32),
                 pltpu.VMEM((lats, 2 * lats), f32),
-                pltpu.VMEM((devices, 1, lats), f32),
+                pltpu.VMEM((devices, 1, 8 * lons), f32),
                 dma((quarter,)),
                 dma((3,)),
                 dma((STEPS, 2, quarter)),

time: 53.8 us -> 53.8 us (level)
  no operation moved by 1% of the time
where the time goes in v7:
time: 53.8 us; the launch traced here: 53.7 us
  Pallas kernels  53.1 us (99%)
  between operations  0.64 us (1%)
    pallas_call x1, Pallas kernels, per_device(): pl.pallas_call(functools.partial(window_kernel, (devices, quarter, freqs,...  50.9 us
    pallas_call x1, Pallas kernels, per_device(): pl.pallas_call(functools.partial(output_kernel, (devices, lons, lats)), o...  2.23 us

profile of v7, /device:TPU:37, one launch (start us, length us, event | category | flops | bytes accessed | tf_op | source)
XLA Modules:
  0.0 53.7 jit_solution(7188859436743605065)
XLA Ops:
  0.6 50.9 %shard_map.59 = (f32[4,9,256,128]{3,2,1,0:T(8,128)S(1)}, f32[64,1,64]{2,1,0:T(1,128)S(1)}) custom-call(f32[4,9,256,128]{3,2,1,0:T(8,128)} %bitcast.3, f32[2,8,128]{2,1,0:T(8,128)} %wind.1, s32[8,128]{1,0:T(8,128)} %land.1, s32[1,128]{1,0:T(1,128)} %bitcast.4), custom_call_target="tpu_custom_call" | custom-call | tf_op jit(solution)/shard_map/pallas_call | solution.py:441
  51.5 2.2 %shard_map.60 = (f32[4,9,256,128]{3,2,1,0:T(8,128)}, f32[4,2,512]{2,1,0:T(2,128)}) custom-call(f32[4,9,256,128]{3,2,1,0:T(8,128)S(1)} %get-tuple-element.6.spectrum, f32[64,1,64]{2,1,0:T(1,128)S(1)} %get-tuple-element.7.arrived), custom_call_target="tpu_custom_call" | custom-call | tf_op jit(solution)/shard_map/pallas_call | solution.py:495

commit v8 on v7

--- a/solution.py
+++ b/solution.py
@@ -29,6 +29,7 @@
 def window_kernel(
     sizes,
     spectrum,
+    columns,
     wind,
     land,
     band,
@@ -56,6 +57,7 @@
     turned,
     message,
     load_sem,
+    bound_sem,
     small_sem,
     halo_send_sem,
     halo_recv_sem,
@@ -86,6 +88,19 @@
     for copy in small:
         copy.start()
 
+    bounds = [
+        pltpu.make_async_copy(
+            columns.at[q, :, :, lon], to.at[0, :, pl.ds(half * freqs, freqs)], bound_sem.at[q]
+        )
+        for q, to, half, lon in (
+            (0, send_e, 0, lons - 1),
+            (1, send_w, 0, 0),
+            (2, send_w, 1, 0),
+            (3, send_e, 1, lons - 1),
+        )
+    ]
+    for copy in bounds:
+        copy.start()
     for k in range(quarter):
         load(k).start()
 
@@ -157,10 +172,11 @@
         halo_copy(s, k, False).start()
 
     with jax.named_scope("first_ship"):
+        for copy in bounds:
+            copy.wait()
+
         @pl.loop(0, quarter)
         def _(k):
-            load(k).wait()
-            pack(0, k)
             ship(0, k)
 
     for copy in small:
@@ -196,6 +212,7 @@
         else:
             inner = [x_rates[q] * (1.0 - (first_row, last_row)[sides[q]]) for q in range(4)]
             if s == 0:
+                load(k).wait()
 
                 @pl.when(k == HEARD[0][1])
                 def _():
@@ -444,7 +461,7 @@
                 pltpu.VMEM((4, quarter, tiles, lats), f32),
                 pltpu.VMEM((devices, 1, 8 * lons), f32),
             ),
-            in_specs=[hbm_space] * 4,
+            in_specs=[hbm_space] * 5,
             out_specs=(vmem_space, vmem_space),
             scratch_shapes=[
                 pltpu.VMEM((4, quarter, tiles, lats), f32),
@@ -469,6 +486,7 @@
                 pltpu.VMEM((lats, 2 * lats), f32),
                 pltpu.VMEM((devices, 1, 8 * lons), f32),
                 dma((quarter,)),
+                dma((4,)),
                 dma((3,)),
                 dma((STEPS, 2, quarter)),
                 dma((STEPS, 2, quarter)),
@@ -486,6 +504,7 @@
                 pltpu.with_memory_space_constraint(argument, pltpu.HBM)
                 for argument in (
                     spectrum.reshape(4, quarter, tiles, lats),
+                    spectrum.reshape(4, quarter, freqs, lons, lats),
                     wind,
                     land_sea,
                     band_rows.reshape(1, lats),

time: 53.8 us -> 53.8 us (level)
  no operation moved by 1% of the time
where the time goes in v8:
time: 53.8 us; the launch traced here: 53.7 us
  Pallas kernels  53.1 us (99%)
  between operations  0.64 us (1%)
    pallas_call x1, Pallas kernels, per_device(): pl.pallas_call(functools.partial(window_kernel, (devices, quarter, freqs,...  50.9 us
    pallas_call x1, Pallas kernels, per_device(): pl.pallas_call(functools.partial(output_kernel, (devices, lons, lats)), o...  2.23 us

profile of v8, /device:TPU:37, one launch (start us, length us, event | category | flops | bytes accessed | tf_op | source)
XLA Modules:
  0.0 53.7 jit_solution(13447344760878954161)
XLA Ops:
  0.6 50.9 %shard_map.59 = (f32[4,9,256,128]{3,2,1,0:T(8,128)S(1)}, f32[64,1,64]{2,1,0:T(1,128)S(1)}) custom-call(f32[4,9,256,128]{3,2,1,0:T(8,128)} %bitcast.4, f32[4,9,32,8,128]{4,3,2,1,0:T(8,128)} %bitcast.5, f32[2,8,128]{2,1,0:T(8,128)} %wind.1, s32[8,128]{1,0:T(8,128)} %land.1, s32[1,128]{1,0:T(1,128)} %bitcast.6), custom_call_target="tpu_custom_call" | custom-call | tf_op jit(solution)/shard_map/pallas_call | solution.py:458
  51.5 2.2 %shard_map.60 = (f32[4,9,256,128]{3,2,1,0:T(8,128)}, f32[4,2,512]{2,1,0:T(2,128)}) custom-call(f32[4,9,256,128]{3,2,1,0:T(8,128)S(1)} %get-tuple-element.6.spectrum, f32[64,1,64]{2,1,0:T(1,128)S(1)} %get-tuple-element.7.arrived), custom_call_target="tpu_custom_call" | custom-call | tf_op jit(solution)/shard_map/pallas_call | solution.py:514
